TPU v7x, 128 devices: a whole 4x4x4 slice. The times are simulated.
128 devices in a mesh: dp: 1, sp: 64 (over z, y, x), tp: 2 (over core).
Axes of the slice: x: 4, y: 4, z: 4, core: 2. Of those that a mesh axis runs over, the one named last changes fastest.
Arguments:
- tokens: bfloat16 [131072, 2688], P(('dp', 'sp', 'tp'))
- w_in: bfloat16 [2688, 10304], P(None, 'tp')
- conv_w: bfloat16 [4, 8, 768], P(None, 'tp')
- conv_bias: bfloat16 [8, 768], P('tp')
- a_log: float32 [64], P('tp')
- dt_bias: float32 [64], P('tp')
- d_skip: float32 [64], P('tp')
- norm_w: bfloat16 [4096], P('tp')
- w_out: bfloat16 [4096, 2688], P('tp')
Outputs:
- output: bfloat16 [131072, 2688], P(('dp', 'sp', 'tp'))
All inputs are finite; a program needn't handle non-finite values.
Results may differ from a plain program's by a relative error of at most 0.0146417.
Values are sent between devices in bfloat16 or wider.
A program may use at most 1 GiB of HBM per device.

v0:
```python
import jax
import jax.numpy as jnp
from jax import lax
from jax.sharding import PartitionSpec as P

SEG_LEN = 256
NORM_EPS = 1e-5


def local_ssd(x_heads, b_mat, c_mat, dt_step, a_log, seg_len):
    seq_blk, n_groups, head_rep, head_dim = x_heads.shape
    n_state = b_mat.shape[-1]
    n_segs = seq_blk // seg_len
    seg_shape = (n_segs, seg_len, n_groups)
    log_decay = -jnp.exp(a_log).reshape(n_groups, head_rep) * dt_step
    cum_log = jnp.cumsum(log_decay.reshape(seg_shape + (head_rep,)), axis=1)
    u_segs = (x_heads * dt_step[..., None]).reshape(seg_shape + (head_rep, head_dim))
    b_segs = b_mat.reshape(seg_shape + (n_state,))
    c_segs = c_mat.reshape(seg_shape + (n_state,))
    causal = jnp.arange(seg_len)[:, None] >= jnp.arange(seg_len)[None, :]
    cum_t = jnp.moveaxis(cum_log, 1, -1)
    weights = jnp.exp(jnp.where(causal, cum_t[..., :, None] - cum_t[..., None, :], -jnp.inf))
    c_dot_b = jnp.einsum("cqgn,cvgn->cgqv", c_segs, b_segs, preferred_element_type=jnp.float32)
    y_diag = jnp.einsum("cgrqv,cvgrp->cqgrp", c_dot_b[:, :, None] * weights, u_segs, preferred_element_type=jnp.float32)
    seg_tot = cum_log[:, -1]
    end_w = jnp.exp(seg_tot[:, None] - cum_log)
    states = jnp.einsum("cvgn,cvgrp->cgrpn", b_segs, u_segs * end_w[..., None], preferred_element_type=jnp.float32)
    inclusive = jnp.cumsum(seg_tot, axis=0)
    exclusive = inclusive - seg_tot
    earlier = jnp.arange(n_segs)[:, None] > jnp.arange(n_segs)[None, :]
    cross_w = jnp.exp(jnp.where(earlier[:, :, None, None], exclusive[:, None] - inclusive[None, :], -jnp.inf))
    starts = jnp.einsum("cjgr,jgrpn->cgrpn", cross_w, states, preferred_element_type=jnp.float32)
    end_state = jnp.einsum("jgr,jgrpn->grpn", jnp.exp(inclusive[-1] - inclusive), states, preferred_element_type=jnp.float32)
    return y_diag, cum_log, c_segs, exclusive, starts, end_state, jnp.exp(inclusive[-1])


def solution(mesh):
    sp_size = mesh.shape["sp"]
    chain_perm = [(src_idx, src_idx + 1) for src_idx in range(sp_size - 1)]
    row_spec = P(("dp", "sp", "tp"), None)

    def layer_block(tokens, w_in, conv_w, conv_bias, a_log, dt_bias, d_skip, norm_w, w_out):
        n_groups, conv_cols = conv_bias.shape
        n_heads = a_log.shape[0]
        inner_dim = norm_w.shape[0]
        head_rep = n_heads // n_groups
        group_inner = inner_dim // n_groups
        head_dim = inner_dim // n_heads
        n_state = (conv_cols - group_inner) // 2
        n_taps = conv_w.shape[0]
        block = lax.all_gather(tokens, "tp", axis=0, tiled=True)
        seq_blk = block.shape[0]
        projected = jnp.dot(block, w_in, preferred_element_type=jnp.float32).astype(jnp.bfloat16)
        projected = projected.reshape(seq_blk, n_groups, -1)
        gate_z = projected[:, :, :group_inner]
        conv_in = projected[:, :, group_inner:group_inner + conv_cols]
        dt_raw = projected[:, :, group_inner + conv_cols:]
        halo = lax.ppermute(conv_in[seq_blk - n_taps + 1:], "sp", chain_perm)
        padded = jnp.concatenate([halo, conv_in], axis=0)
        conv_wf = conv_w.astype(jnp.float32)
        conv_acc = conv_bias.astype(jnp.float32) + padded[:seq_blk] * conv_wf[0]
        for tap_idx in range(1, n_taps):
            conv_acc = conv_acc + padded[tap_idx:tap_idx + seq_blk] * conv_wf[tap_idx]
        activated = jax.nn.silu(conv_acc).astype(jnp.bfloat16)
        x_heads = activated[:, :, :group_inner].reshape(seq_blk, n_groups, head_rep, head_dim)
        b_mat = activated[:, :, group_inner:group_inner + n_state]
        c_mat = activated[:, :, group_inner + n_state:]
        dt_step = jax.nn.softplus(dt_raw.astype(jnp.float32).reshape(seq_blk, n_heads) + dt_bias).reshape(seq_blk, n_groups, head_rep)
        y_diag, cum_log, c_segs, exclusive, starts, end_state, blk_decay = local_ssd(x_heads, b_mat, c_mat, dt_step, a_log, SEG_LEN)

        def chain_hop(hop_idx, state_in):
            return lax.ppermute(blk_decay[..., None, None] * state_in + end_state, "sp", chain_perm)

        incoming = lax.fori_loop(0, sp_size - 1, chain_hop, jnp.zeros_like(end_state))
        starts = starts + jnp.exp(exclusive)[..., None, None] * incoming
        y_off = jnp.exp(cum_log)[..., None] * jnp.einsum("cqgn,cgrpn->cqgrp", c_segs, starts, preferred_element_type=jnp.float32)
        y_ssd = (y_diag + y_off).reshape(seq_blk, n_groups, head_rep, head_dim) + d_skip.reshape(n_groups, head_rep)[:, :, None] * x_heads
        y_gated = y_ssd.reshape(seq_blk, n_groups, group_inner) * jax.nn.silu(gate_z.astype(jnp.float32))
        inv_rms = lax.rsqrt(jnp.mean(y_gated * y_gated, axis=-1, keepdims=True) + NORM_EPS)
        y_normed = (y_gated * inv_rms * norm_w.astype(jnp.float32).reshape(n_groups, group_inner)).astype(jnp.bfloat16)
        partial_out = jnp.dot(y_normed.reshape(seq_blk, inner_dim), w_out, preferred_element_type=jnp.float32).astype(jnp.bfloat16)
        reduced = lax.psum_scatter(partial_out, "tp", scatter_dimension=0, tiled=True)
        return (tokens.astype(jnp.float32) + reduced.astype(jnp.float32)).astype(jnp.bfloat16)

    return jax.shard_map(
        layer_block,
        mesh=mesh,
        in_specs=(row_spec, P(None, "tp"), P(None, "tp", None), P("tp", None), P("tp"), P("tp"), P("tp"), P("tp"), P("tp", None)),
        out_specs=row_spec,
        check_vma=False)
```

profile of v0, /device:TPU:1, one launch (start us, length us, event | category | flops | bytes accessed | tf_op | source)
XLA Modules:
  0.0 2189.4 jit_solution(9257615178486055109)
XLA Ops:
  15.5 24.0 %all-gather.2.cloned.1.call-done = bf16[2048,2688]{1,0:T(8,128)(2,1)} async-done(((bf16[1024,2688]{1,0:T(8,128)(2,1)}), bf16[2048,2688]{1,0:T(8,128)(2,1)}) %all-gather.2.cloned.1.call-update) | async-done | bytes 11010064 | tf_op jit(solution)/shard_map/all_gather | solution.py:51
  39.5 68.9 %convolution_convert_fusion = bf16[2048,5152]{0,1:T(8,128)(2,1)} fusion(bf16[2048,2688]{1,0:T(8,128)(2,1)} %all-gather.2.cloned.1.call-done, bf16[2688,5152]{0,1:T(8,128)(2,1)} %param.12), kind=kOutput, calls=%fused_computation.12 | convolution fusion | flops 56734318592 | bytes 59809792 | tf_op jit(solution)/shard_map/dot_general | solution.py:53
  202.1 23.2 %multiply_convert_fusion = bf16[2048,4,768]{2,0,1:T(8,128)(2,1)S(1)} fusion(bf16[2048,4,768]{2,0,1:T(8,128)(2,1)} %copy.101, bf16[3,4,768]{2,0,1:T(4,128)(2,1)S(1)} %collective-permute-done.1, f32[4,768]{1,0:T(4,128)S(1)} %copy-done.5, f32[4,768]{1,0:T(4,128)S(1)} %copy-done.6, f32[4,768]{1,0:T(4,128)S(1)} %copy-done.7, f32[4,768]{1,0:T(4,128)S(1)} %copy-done.4, ...), kind=kLoop, calls=%fused_computation.11 | loop fusion | flops 163577856 | bytes 25245696 | tf_op jit(solution)/shard_map/convert_element_type | solution.py:64
  293.4 20.4 fusion
  313.9 1572.1 %while.10 = (s32[]{:T(128)}, f32[4,8,64,128]{3,2,1,0:T(8,128)S(1)}, f32[4,8]{1,0:T(4,128)S(1)}, f32[4,8,64,128]{3,2,1,0:T(8,128)S(1)}, s32[]{:T(128)}) while((s32[]{:T(128)}, f32[4,8,64,128]{3,2,1,0:T(8,128)S(1)}, f32[4,8]{1,0:T(4,128)S(1)}, f32[4,8,64,128]{3,2,1,0:T(8,128)S(1)}, s32[]{:T(128)}) %tuple.35), condition=%wide.region_4.5_spmd, body=%wide.region_3.4_spmd.sunk | while | flops 524290 | bytes 7340261 | solution.py:74
  317.3 21.9 %collective-permute-done = f32[4,8,64,128]{3,2,1,0:T(8,128)S(1)} collective-permute-done((f32[4,8,64,128]{3,2,1,0:T(8,128)S(1)}, f32[4,8,64,128]{3,2,1,0:T(8,128)S(1)}, u32[]{:S(2)}, u32[]{:S(2)}) %collective-permute-start) | collective-permute-done | bytes 1048608 | tf_op jit(solution)/shard_map/while/body/eval_jaxpr/ppermute | solution.py:72
  343.6 21.1 collective-permute-done
  369.0 20.2 collective-permute-done
  393.6 19.4 collective-permute-done
  666.6 19.1 collective-permute-done
  692.4 19.9 collective-permute-done
  719.1 20.8 collective-permute-done
  746.7 21.7 collective-permute-done
  775.2 22.6 %collective-permute-done = f32[4,8,64,128]{3,2,1,0:T(8,128)S(1)} collective-permute-done((f32[4,8,64,128]{3,2,1,0:T(8,128)S(1)}, f32[4,8,64,128]{3,2,1,0:T(8,128)S(1)}, u32[]{:S(2)}, u32[]{:S(2)}) %collective-permute-start) | collective-permute-done | bytes 1048608 | tf_op jit(solution)/shard_map/while/body/eval_jaxpr/ppermute | solution.py:72
  804.7 22.3 %collective-permute-done = f32[4,8,64,128]{3,2,1,0:T(8,128)S(1)} collective-permute-done((f32[4,8,64,128]{3,2,1,0:T(8,128)S(1)}, f32[4,8,64,128]{3,2,1,0:T(8,128)S(1)}, u32[]{:S(2)}, u32[]{:S(2)}) %collective-permute-start) | collective-permute-done | bytes 1048608 | tf_op jit(solution)/shard_map/while/body/eval_jaxpr/ppermute | solution.py:72
  833.6 21.3 collective-permute-done
  860.4 20.1 collective-permute-done
  886.5 19.0 collective-permute-done
  1334.7 18.6 collective-permute-done
  1360.0 18.9 collective-permute-done
  1393.2 20.7 collective-permute-done
  1420.7 21.6 collective-permute-done
  1449.1 22.5 %collective-permute-done = f32[4,8,64,128]{3,2,1,0:T(8,128)S(1)} collective-permute-done((f32[4,8,64,128]{3,2,1,0:T(8,128)S(1)}, f32[4,8,64,128]{3,2,1,0:T(8,128)S(1)}, u32[]{:S(2)}, u32[]{:S(2)}) %collective-permute-start) | collective-permute-done | bytes 1048608 | tf_op jit(solution)/shard_map/while/body/eval_jaxpr/ppermute | solution.py:72
  1483.5 21.7 collective-permute-done
  1515.3 20.7 collective-permute-done
  1541.5 19.4 collective-permute-done
  1568.2 18.5 collective-permute-done
  1720.7 30.8 %collective-permute-start = (f32[4,8,64,128]{3,2,1,0:T(8,128)S(1)}, f32[4,8,64,128]{3,2,1,0:T(8,128)S(1)}, u32[]{:S(2)}, u32[]{:S(2)}) collective-permute-start(f32[4,8,64,128]{3,2,1,0:T(8,128)S(1)} %multiply_add_fusion.2), channel_id=1, source_target_pairs={{0,2},{2,4},{4,6},{6,8},{8,10},{10,12},{12,14},{14,16},{16,18},{18... | collective-permute-start | bytes 3145736 | tf_op jit(solution)/shard_map/while/body/eval_jaxpr/ppermute | solution.py:72
  1909.1 23.1 %copy.98 = f32[8,256,4,8,64]{4,3,1,0,2:T(8,128)} copy(f32[8,256,4,8,64]{1,4,3,2,0:T(8,128)} %fusion.14) | data formatting | bytes 33554432 | tf_op jit(solution)/shard_map/reshape | solution.py:77
  1932.2 27.6 %reshape.126 = f32[2048,4,512]{2,0,1:T(8,128)} reshape(f32[8,256,4,8,64]{4,3,1,0,2:T(8,128)} %copy.98) | data formatting | bytes 33554432 | tf_op jit(solution)/shard_map/reshape | solution.py:77
  1988.4 31.5 %convolution_convert_fusion.1 = bf16[2048,2688]{1,0:T(8,128)(2,1)} fusion(bf16[2048,2048]{0,1:T(8,128)(2,1)} %bitcast.102, bf16[2048,2688]{1,0:T(8,128)(2,1)} %param.19), kind=kOutput, calls=%fused_computation.31 | convolution fusion | flops 22554083328 | bytes 30408704 | tf_op jit(solution)/shard_map/dot_general | solution.py:81
  2020.0 154.2 %reduce-scatter.2.cloned.1.call-done = bf16[1024,2688]{1,0:T(8,128)(2,1)} async-done(((bf16[2048,2688]{1,0:T(8,128)(2,1)}), bf16[1024,2688]{1,0:T(8,128)(2,1)}) %reduce-scatter.2.cloned.1.call-update) | async-done | bytes 5505040 | tf_op jit(solution)/shard_map/reduce_scatter | solution.py:82
  (257 shorter events, 1317.9 us)
Async XLA Ops:
  6.5 32.9 %all-gather.2.cloned.1.call-start = ((), (), s32[]{:S(2)}) async-start(), calls=%async_computation.1 | async-start | bytes 16515072 | tf_op jit(solution)/shard_map/all_gather | solution.py:51
  7.3 2166.9 %reduce-scatter.2.cloned.1.call-start = ((), (), s32[]{:S(2)}) async-start(), calls=%async_computation.2 | async-start | bytes 16515072 | tf_op jit(solution)/shard_map/reduce_scatter | solution.py:82
  144.3 57.8 %collective-permute-start.1 = (bf16[3,4,768]{2,0,1:T(4,128)(2,1)S(1)}, bf16[3,4,768]{2,0,1:T(4,128)(2,1)S(1)}, u32[]{:S(2)}, u32[]{:S(2)}) collective-permute-start(bf16[3,4,768]{2,0,1:T(4,128)(2,1)S(1)} %copy.100), channel_id=1, source_target_pairs={{0,2},{2,4},{4,6},{6,8},{8,10},{10,12},{12,14},{14,16},{16,18},{18... | collective-permute-start | bytes 55304 | tf_op jit(solution)/shard_map/ppermute | solution.py:58
  314.1 25.1 %collective-permute-start = (f32[4,8,64,128]{3,2,1,0:T(8,128)S(1)}, f32[4,8,64,128]{3,2,1,0:T(8,128)S(1)}, u32[]{:S(2)}, u32[]{:S(2)}) collective-permute-start(f32[4,8,64,128]{3,2,1,0:T(8,128)S(1)} %multiply_add_fusion.2), channel_id=1, source_target_pairs={{0,2},{2,4},{4,6},{6,8},{8,10},{10,12},{12,14},{14,16},{16,18},{18... | collective-permute-start | bytes 3145736 | tf_op jit(solution)/shard_map/while/body/eval_jaxpr/ppermute | solution.py:72
  339.4 25.3 %collective-permute-start = (f32[4,8,64,128]{3,2,1,0:T(8,128)S(1)}, f32[4,8,64,128]{3,2,1,0:T(8,128)S(1)}, u32[]{:S(2)}, u32[]{:S(2)}) collective-permute-start(f32[4,8,64,128]{3,2,1,0:T(8,128)S(1)} %multiply_add_fusion.2), channel_id=1, source_target_pairs={{0,2},{2,4},{4,6},{6,8},{8,10},{10,12},{12,14},{14,16},{16,18},{18... | collective-permute-start | bytes 3145736 | tf_op jit(solution)/shard_map/while/body/eval_jaxpr/ppermute | solution.py:72
  609.4 25.9 %collective-permute-start = (f32[4,8,64,128]{3,2,1,0:T(8,128)S(1)}, f32[4,8,64,128]{3,2,1,0:T(8,128)S(1)}, u32[]{:S(2)}, u32[]{:S(2)}) collective-permute-start(f32[4,8,64,128]{3,2,1,0:T(8,128)S(1)} %multiply_add_fusion.2), channel_id=1, source_target_pairs={{0,2},{2,4},{4,6},{6,8},{8,10},{10,12},{12,14},{14,16},{16,18},{18... | collective-permute-start | bytes 3145736 | tf_op jit(solution)/shard_map/while/body/eval_jaxpr/ppermute | solution.py:72
  660.0 25.7 %collective-permute-start = (f32[4,8,64,128]{3,2,1,0:T(8,128)S(1)}, f32[4,8,64,128]{3,2,1,0:T(8,128)S(1)}, u32[]{:S(2)}, u32[]{:S(2)}) collective-permute-start(f32[4,8,64,128]{3,2,1,0:T(8,128)S(1)} %multiply_add_fusion.2), channel_id=1, source_target_pairs={{0,2},{2,4},{4,6},{6,8},{8,10},{10,12},{12,14},{14,16},{16,18},{18... | collective-permute-start | bytes 3145736 | tf_op jit(solution)/shard_map/while/body/eval_jaxpr/ppermute | solution.py:72
  685.8 26.5 %collective-permute-start = (f32[4,8,64,128]{3,2,1,0:T(8,128)S(1)}, f32[4,8,64,128]{3,2,1,0:T(8,128)S(1)}, u32[]{:S(2)}, u32[]{:S(2)}) collective-permute-start(f32[4,8,64,128]{3,2,1,0:T(8,128)S(1)} %multiply_add_fusion.2), channel_id=1, source_target_pairs={{0,2},{2,4},{4,6},{6,8},{8,10},{10,12},{12,14},{14,16},{16,18},{18... | collective-permute-start | bytes 3145736 | tf_op jit(solution)/shard_map/while/body/eval_jaxpr/ppermute | solution.py:72
  712.5 27.4 %collective-permute-start = (f32[4,8,64,128]{3,2,1,0:T(8,128)S(1)}, f32[4,8,64,128]{3,2,1,0:T(8,128)S(1)}, u32[]{:S(2)}, u32[]{:S(2)}) collective-permute-start(f32[4,8,64,128]{3,2,1,0:T(8,128)S(1)} %multiply_add_fusion.2), channel_id=1, source_target_pairs={{0,2},{2,4},{4,6},{6,8},{8,10},{10,12},{12,14},{14,16},{16,18},{18... | collective-permute-start | bytes 3145736 | tf_op jit(solution)/shard_map/while/body/eval_jaxpr/ppermute | solution.py:72
  740.1 28.3 %collective-permute-start = (f32[4,8,64,128]{3,2,1,0:T(8,128)S(1)}, f32[4,8,64,128]{3,2,1,0:T(8,128)S(1)}, u32[]{:S(2)}, u32[]{:S(2)}) collective-permute-start(f32[4,8,64,128]{3,2,1,0:T(8,128)S(1)} %multiply_add_fusion.2), channel_id=1, source_target_pairs={{0,2},{2,4},{4,6},{6,8},{8,10},{10,12},{12,14},{14,16},{16,18},{18... | collective-permute-start | bytes 3145736 | tf_op jit(solution)/shard_map/while/body/eval_jaxpr/ppermute | solution.py:72
  768.6 29.2 %collective-permute-start = (f32[4,8,64,128]{3,2,1,0:T(8,128)S(1)}, f32[4,8,64,128]{3,2,1,0:T(8,128)S(1)}, u32[]{:S(2)}, u32[]{:S(2)}) collective-permute-start(f32[4,8,64,128]{3,2,1,0:T(8,128)S(1)} %multiply_add_fusion.2), channel_id=1, source_target_pairs={{0,2},{2,4},{4,6},{6,8},{8,10},{10,12},{12,14},{14,16},{16,18},{18... | collective-permute-start | bytes 3145736 | tf_op jit(solution)/shard_map/while/body/eval_jaxpr/ppermute | solution.py:72
  798.0 28.9 %collective-permute-start = (f32[4,8,64,128]{3,2,1,0:T(8,128)S(1)}, f32[4,8,64,128]{3,2,1,0:T(8,128)S(1)}, u32[]{:S(2)}, u32[]{:S(2)}) collective-permute-start(f32[4,8,64,128]{3,2,1,0:T(8,128)S(1)} %multiply_add_fusion.2), channel_id=1, source_target_pairs={{0,2},{2,4},{4,6},{6,8},{8,10},{10,12},{12,14},{14,16},{16,18},{18... | collective-permute-start | bytes 3145736 | tf_op jit(solution)/shard_map/while/body/eval_jaxpr/ppermute | solution.py:72
  827.1 27.9 %collective-permute-start = (f32[4,8,64,128]{3,2,1,0:T(8,128)S(1)}, f32[4,8,64,128]{3,2,1,0:T(8,128)S(1)}, u32[]{:S(2)}, u32[]{:S(2)}) collective-permute-start(f32[4,8,64,128]{3,2,1,0:T(8,128)S(1)} %multiply_add_fusion.2), channel_id=1, source_target_pairs={{0,2},{2,4},{4,6},{6,8},{8,10},{10,12},{12,14},{14,16},{16,18},{18... | collective-permute-start | bytes 3145736 | tf_op jit(solution)/shard_map/while/body/eval_jaxpr/ppermute | solution.py:72
  855.1 25.3 %collective-permute-start = (f32[4,8,64,128]{3,2,1,0:T(8,128)S(1)}, f32[4,8,64,128]{3,2,1,0:T(8,128)S(1)}, u32[]{:S(2)}, u32[]{:S(2)}) collective-permute-start(f32[4,8,64,128]{3,2,1,0:T(8,128)S(1)} %multiply_add_fusion.2), channel_id=1, source_target_pairs={{0,2},{2,4},{4,6},{6,8},{8,10},{10,12},{12,14},{14,16},{16,18},{18... | collective-permute-start | bytes 3145736 | tf_op jit(solution)/shard_map/while/body/eval_jaxpr/ppermute | solution.py:72
  880.6 24.8 %collective-permute-start = (f32[4,8,64,128]{3,2,1,0:T(8,128)S(1)}, f32[4,8,64,128]{3,2,1,0:T(8,128)S(1)}, u32[]{:S(2)}, u32[]{:S(2)}) collective-permute-start(f32[4,8,64,128]{3,2,1,0:T(8,128)S(1)} %multiply_add_fusion.2), channel_id=1, source_target_pairs={{0,2},{2,4},{4,6},{6,8},{8,10},{10,12},{12,14},{14,16},{16,18},{18... | collective-permute-start | bytes 3145736 | tf_op jit(solution)/shard_map/while/body/eval_jaxpr/ppermute | solution.py:72
  1105.1 26.7 %collective-permute-start = (f32[4,8,64,128]{3,2,1,0:T(8,128)S(1)}, f32[4,8,64,128]{3,2,1,0:T(8,128)S(1)}, u32[]{:S(2)}, u32[]{:S(2)}) collective-permute-start(f32[4,8,64,128]{3,2,1,0:T(8,128)S(1)} %multiply_add_fusion.2), channel_id=1, source_target_pairs={{0,2},{2,4},{4,6},{6,8},{8,10},{10,12},{12,14},{14,16},{16,18},{18... | collective-permute-start | bytes 3145736 | tf_op jit(solution)/shard_map/while/body/eval_jaxpr/ppermute | solution.py:72
  1132.0 24.5 %collective-permute-start = (f32[4,8,64,128]{3,2,1,0:T(8,128)S(1)}, f32[4,8,64,128]{3,2,1,0:T(8,128)S(1)}, u32[]{:S(2)}, u32[]{:S(2)}) collective-permute-start(f32[4,8,64,128]{3,2,1,0:T(8,128)S(1)} %multiply_add_fusion.2), channel_id=1, source_target_pairs={{0,2},{2,4},{4,6},{6,8},{8,10},{10,12},{12,14},{14,16},{16,18},{18... | collective-permute-start | bytes 3145736 | tf_op jit(solution)/shard_map/while/body/eval_jaxpr/ppermute | solution.py:72
  1248.2 25.5 %collective-permute-start = (f32[4,8,64,128]{3,2,1,0:T(8,128)S(1)}, f32[4,8,64,128]{3,2,1,0:T(8,128)S(1)}, u32[]{:S(2)}, u32[]{:S(2)}) collective-permute-start(f32[4,8,64,128]{3,2,1,0:T(8,128)S(1)} %multiply_add_fusion.2), channel_id=1, source_target_pairs={{0,2},{2,4},{4,6},{6,8},{8,10},{10,12},{12,14},{14,16},{16,18},{18... | collective-permute-start | bytes 3145736 | tf_op jit(solution)/shard_map/while/body/eval_jaxpr/ppermute | solution.py:72
  1273.9 29.5 %collective-permute-start = (f32[4,8,64,128]{3,2,1,0:T(8,128)S(1)}, f32[4,8,64,128]{3,2,1,0:T(8,128)S(1)}, u32[]{:S(2)}, u32[]{:S(2)}) collective-permute-start(f32[4,8,64,128]{3,2,1,0:T(8,128)S(1)} %multiply_add_fusion.2), channel_id=1, source_target_pairs={{0,2},{2,4},{4,6},{6,8},{8,10},{10,12},{12,14},{14,16},{16,18},{18... | collective-permute-start | bytes 3145736 | tf_op jit(solution)/shard_map/while/body/eval_jaxpr/ppermute | solution.py:72
  1326.3 27.0 %collective-permute-start = (f32[4,8,64,128]{3,2,1,0:T(8,128)S(1)}, f32[4,8,64,128]{3,2,1,0:T(8,128)S(1)}, u32[]{:S(2)}, u32[]{:S(2)}) collective-permute-start(f32[4,8,64,128]{3,2,1,0:T(8,128)S(1)} %multiply_add_fusion.2), channel_id=1, source_target_pairs={{0,2},{2,4},{4,6},{6,8},{8,10},{10,12},{12,14},{14,16},{16,18},{18... | collective-permute-start | bytes 3145736 | tf_op jit(solution)/shard_map/while/body/eval_jaxpr/ppermute | solution.py:72
  1353.5 25.4 %collective-permute-start = (f32[4,8,64,128]{3,2,1,0:T(8,128)S(1)}, f32[4,8,64,128]{3,2,1,0:T(8,128)S(1)}, u32[]{:S(2)}, u32[]{:S(2)}) collective-permute-start(f32[4,8,64,128]{3,2,1,0:T(8,128)S(1)} %multiply_add_fusion.2), channel_id=1, source_target_pairs={{0,2},{2,4},{4,6},{6,8},{8,10},{10,12},{12,14},{14,16},{16,18},{18... | collective-permute-start | bytes 3145736 | tf_op jit(solution)/shard_map/while/body/eval_jaxpr/ppermute | solution.py:72
  1379.1 34.8 %collective-permute-start = (f32[4,8,64,128]{3,2,1,0:T(8,128)S(1)}, f32[4,8,64,128]{3,2,1,0:T(8,128)S(1)}, u32[]{:S(2)}, u32[]{:S(2)}) collective-permute-start(f32[4,8,64,128]{3,2,1,0:T(8,128)S(1)} %multiply_add_fusion.2), channel_id=1, source_target_pairs={{0,2},{2,4},{4,6},{6,8},{8,10},{10,12},{12,14},{14,16},{16,18},{18... | collective-permute-start | bytes 3145736 | tf_op jit(solution)/shard_map/while/body/eval_jaxpr/ppermute | solution.py:72
  1414.1 28.3 %collective-permute-start = (f32[4,8,64,128]{3,2,1,0:T(8,128)S(1)}, f32[4,8,64,128]{3,2,1,0:T(8,128)S(1)}, u32[]{:S(2)}, u32[]{:S(2)}) collective-permute-start(f32[4,8,64,128]{3,2,1,0:T(8,128)S(1)} %multiply_add_fusion.2), channel_id=1, source_target_pairs={{0,2},{2,4},{4,6},{6,8},{8,10},{10,12},{12,14},{14,16},{16,18},{18... | collective-permute-start | bytes 3145736 | tf_op jit(solution)/shard_map/while/body/eval_jaxpr/ppermute | solution.py:72
  1442.5 29.1 %collective-permute-start = (f32[4,8,64,128]{3,2,1,0:T(8,128)S(1)}, f32[4,8,64,128]{3,2,1,0:T(8,128)S(1)}, u32[]{:S(2)}, u32[]{:S(2)}) collective-permute-start(f32[4,8,64,128]{3,2,1,0:T(8,128)S(1)} %multiply_add_fusion.2), channel_id=1, source_target_pairs={{0,2},{2,4},{4,6},{6,8},{8,10},{10,12},{12,14},{14,16},{16,18},{18... | collective-permute-start | bytes 3145736 | tf_op jit(solution)/shard_map/while/body/eval_jaxpr/ppermute | solution.py:72
  1471.8 33.4 %collective-permute-start = (f32[4,8,64,128]{3,2,1,0:T(8,128)S(1)}, f32[4,8,64,128]{3,2,1,0:T(8,128)S(1)}, u32[]{:S(2)}, u32[]{:S(2)}) collective-permute-start(f32[4,8,64,128]{3,2,1,0:T(8,128)S(1)} %multiply_add_fusion.2), channel_id=1, source_target_pairs={{0,2},{2,4},{4,6},{6,8},{8,10},{10,12},{12,14},{14,16},{16,18},{18... | collective-permute-start | bytes 3145736 | tf_op jit(solution)/shard_map/while/body/eval_jaxpr/ppermute | solution.py:72
  1505.3 30.7 %collective-permute-start = (f32[4,8,64,128]{3,2,1,0:T(8,128)S(1)}, f32[4,8,64,128]{3,2,1,0:T(8,128)S(1)}, u32[]{:S(2)}, u32[]{:S(2)}) collective-permute-start(f32[4,8,64,128]{3,2,1,0:T(8,128)S(1)} %multiply_add_fusion.2), channel_id=1, source_target_pairs={{0,2},{2,4},{4,6},{6,8},{8,10},{10,12},{12,14},{14,16},{16,18},{18... | collective-permute-start | bytes 3145736 | tf_op jit(solution)/shard_map/while/body/eval_jaxpr/ppermute | solution.py:72
  1536.2 24.7 %collective-permute-start = (f32[4,8,64,128]{3,2,1,0:T(8,128)S(1)}, f32[4,8,64,128]{3,2,1,0:T(8,128)S(1)}, u32[]{:S(2)}, u32[]{:S(2)}) collective-permute-start(f32[4,8,64,128]{3,2,1,0:T(8,128)S(1)} %multiply_add_fusion.2), channel_id=1, source_target_pairs={{0,2},{2,4},{4,6},{6,8},{8,10},{10,12},{12,14},{14,16},{16,18},{18... | collective-permute-start | bytes 3145736 | tf_op jit(solution)/shard_map/while/body/eval_jaxpr/ppermute | solution.py:72
  1561.1 25.7 %collective-permute-start = (f32[4,8,64,128]{3,2,1,0:T(8,128)S(1)}, f32[4,8,64,128]{3,2,1,0:T(8,128)S(1)}, u32[]{:S(2)}, u32[]{:S(2)}) collective-permute-start(f32[4,8,64,128]{3,2,1,0:T(8,128)S(1)} %multiply_add_fusion.2), channel_id=1, source_target_pairs={{0,2},{2,4},{4,6},{6,8},{8,10},{10,12},{12,14},{14,16},{16,18},{18... | collective-permute-start | bytes 3145736 | tf_op jit(solution)/shard_map/while/body/eval_jaxpr/ppermute | solution.py:72
  1720.7 46.5 %collective-permute-start = (f32[4,8,64,128]{3,2,1,0:T(8,128)S(1)}, f32[4,8,64,128]{3,2,1,0:T(8,128)S(1)}, u32[]{:S(2)}, u32[]{:S(2)}) collective-permute-start(f32[4,8,64,128]{3,2,1,0:T(8,128)S(1)} %multiply_add_fusion.2), channel_id=1, source_target_pairs={{0,2},{2,4},{4,6},{6,8},{8,10},{10,12},{12,14},{14,16},{16,18},{18... | collective-permute-start | bytes 3145736 | tf_op jit(solution)/shard_map/while/body/eval_jaxpr/ppermute | solution.py:72
  1767.4 24.8 %collective-permute-start = (f32[4,8,64,128]{3,2,1,0:T(8,128)S(1)}, f32[4,8,64,128]{3,2,1,0:T(8,128)S(1)}, u32[]{:S(2)}, u32[]{:S(2)}) collective-permute-start(f32[4,8,64,128]{3,2,1,0:T(8,128)S(1)} %multiply_add_fusion.2), channel_id=1, source_target_pairs={{0,2},{2,4},{4,6},{6,8},{8,10},{10,12},{12,14},{14,16},{16,18},{18... | collective-permute-start | bytes 3145736 | tf_op jit(solution)/shard_map/while/body/eval_jaxpr/ppermute | solution.py:72
  1792.3 25.0 %collective-permute-start = (f32[4,8,64,128]{3,2,1,0:T(8,128)S(1)}, f32[4,8,64,128]{3,2,1,0:T(8,128)S(1)}, u32[]{:S(2)}, u32[]{:S(2)}) collective-permute-start(f32[4,8,64,128]{3,2,1,0:T(8,128)S(1)} %multiply_add_fusion.2), channel_id=1, source_target_pairs={{0,2},{2,4},{4,6},{6,8},{8,10},{10,12},{12,14},{14,16},{16,18},{18... | collective-permute-start | bytes 3145736 | tf_op jit(solution)/shard_map/while/body/eval_jaxpr/ppermute | solution.py:72
  1817.5 24.5 %collective-permute-start = (f32[4,8,64,128]{3,2,1,0:T(8,128)S(1)}, f32[4,8,64,128]{3,2,1,0:T(8,128)S(1)}, u32[]{:S(2)}, u32[]{:S(2)}) collective-permute-start(f32[4,8,64,128]{3,2,1,0:T(8,128)S(1)} %multiply_add_fusion.2), channel_id=1, source_target_pairs={{0,2},{2,4},{4,6},{6,8},{8,10},{10,12},{12,14},{14,16},{16,18},{18... | collective-permute-start | bytes 3145736 | tf_op jit(solution)/shard_map/while/body/eval_jaxpr/ppermute | solution.py:72
  (46 other events, 2494.0 us)
Sparse Core Ops, SparseCore 0:
  9.0 30.4 all-gather.1
  2020.1 154.0 reduce-scatter.1
where the time goes:
time: 2200 us; the launch traced here: 2190 us
  waiting for transfers between devices  1300 us (59%)
  starting transfers between devices  443 us (20%)
  local copies, waits for them, and re-layouts  163 us (7%)
  matrix products  158 us (7%)
  other arithmetic  109 us (5%)
    ppermute x63, waiting for transfers between devices, chain_hop(): lax.ppermute(blk_decay[..., None, None] * state_in + end_state, 'sp', cha...  1120 us
    ppermute x63, starting transfers between devices, chain_hop(): lax.ppermute(blk_decay[..., None, None] * state_in + end_state, 'sp', cha...  440 us
    reduce_scatter x1, waiting for transfers between devices, layer_block(): lax.psum_scatter(partial_out, 'tp', scatter_dimension=0, tiled=True)  154 us
    dot_general x1, matrix products, layer_block(): jnp.dot(block, w_in, preferred_element_type=jnp.float32)  68.9 us
    reshape x2, local copies, waits for them, and re-layouts, layer_block(): (y_diag + y_off).reshape(seq_blk, n_groups, head_rep, head_dim)  50.8 us
    unnamed x29, local copies, waits for them, and re-layouts  44.3 us
  transfers between devices with their start and end apart: 66, of which 65 were waited for; matrix products, arithmetic and copies ran while one was open for 3% of the time, Pallas kernels for 0%

commit v1 on v0

v1 whole, which is shorter than its diff:
```python
import functools

import jax
import jax.numpy as jnp
from jax import lax
from jax.experimental import pallas as pl
from jax.experimental.pallas import tpu as pltpu
from jax.sharding import PartitionSpec as P

SEG = 128
NORM_EPS = 1e-5
LANES = 128
PIECE_PAD = 8
LOG2E = 1.4426950408889634
F32 = jnp.float32
BF16 = jnp.bfloat16


def spread(values, one_hot):
    n_heads = LANES // 4
    high = values.astype(BF16)
    rest = values - high.astype(F32)
    mid = rest.astype(BF16)
    low = (rest - mid.astype(F32)).astype(BF16)
    lane = lax.broadcasted_iota(jnp.int32, values.shape, 1)
    parts = jnp.where(lane < n_heads, high.astype(F32), jnp.where(lane < 2 * n_heads, mid.astype(F32), low.astype(F32)))
    parts = jnp.where(lane < 3 * n_heads, parts, 0.0).astype(BF16)
    return jnp.dot(parts, one_hot, preferred_element_type=F32)


def conv_kernel(dims, tp_ref, own_ref, oth_ref, halo_ref, cw_ref, cb_ref, hp_ref, oh_ref,
                z_ref, act_ref, dts_ref, end_ref, ext, state, total):
    n_groups, group_inner, n_state, head_rep, half_segs, n_segs = dims
    conv_cols = group_inner + 2 * n_state
    group_cols = 2 * group_inner + 2 * n_state + head_rep
    seg_idx = pl.program_id(0)
    is_own = (seg_idx // half_segs) == tp_ref[0]

    @pl.when(seg_idx == 0)
    def _():
        state[...] = jnp.zeros_like(state)
        total[...] = jnp.zeros_like(total)
        for g in range(n_groups):
            lo = g * group_cols + group_inner
            ext[g, 0:8] = halo_ref[:, lo:lo + conv_cols].astype(F32)[-8:]

    def rows(lo, width):
        return jnp.where(is_own, own_ref[:, lo:lo + width], oth_ref[:, lo:lo + width])

    dt_raw = jnp.concatenate([rows(g * group_cols + group_cols - head_rep, head_rep).astype(F32) for g in range(n_groups)], axis=1)
    dt_raw = jnp.concatenate([dt_raw] * 4, axis=1)
    dt_step = jax.nn.softplus(dt_raw + hp_ref[1:2])
    log_decay = -jnp.exp(hp_ref[0:1]) * dt_step * LOG2E
    row_id = lax.broadcasted_iota(jnp.int32, (SEG, SEG), 0)
    col_id = lax.broadcasted_iota(jnp.int32, (SEG, SEG), 1)
    tri = (row_id >= col_id).astype(F32)
    cum = jnp.dot(tri, log_decay, precision=lax.Precision.HIGHEST, preferred_element_type=F32)
    dts_ref[0] = dt_step
    dts_ref[1] = cum
    seg_total = cum[SEG - 1:SEG]
    total[...] += seg_total
    end_w = spread(jnp.exp2(seg_total - cum) * dt_step, oh_ref[...])
    seg_decay = spread(jnp.exp2(jnp.broadcast_to(seg_total, (8, LANES))), oh_ref[...])[0:1]

    for g in range(n_groups):
        lo = g * group_cols
        z_ref[:, g * group_inner:(g + 1) * group_inner] = rows(lo, group_inner)
        ext[g, 8:8 + SEG] = rows(lo + group_inner, conv_cols).astype(F32)
        c0 = g * conv_cols
        acc = cb_ref[:, c0:c0 + conv_cols] + ext[g, 5:5 + SEG] * cw_ref[0:1, c0:c0 + conv_cols]
        for k in range(1, 4):
            acc = acc + ext[g, 5 + k:5 + k + SEG] * cw_ref[k:k + 1, c0:c0 + conv_cols]
        ext[g, 0:8] = ext[g, SEG:SEG + 8]
        act = (acc / (1.0 + jnp.exp(-acc))).astype(BF16)
        act_ref[:, c0:c0 + conv_cols] = act
        i0, i1 = g * group_inner, (g + 1) * group_inner
        weighted = (act[:, :group_inner].astype(F32) * end_w[:, i0:i1]).astype(BF16)
        b_mat = act[:, group_inner:group_inner + n_state]
        new = lax.dot_general(b_mat, weighted, (((0,), (0,)), ((), ())), preferred_element_type=F32)
        state[:, i0:i1] = state[:, i0:i1] * seg_decay[:, i0:i1] + new

    @pl.when(seg_idx == n_segs - 1)
    def _():
        decay = spread(jnp.exp2(jnp.broadcast_to(total[...], (8, LANES))), oh_ref[...])
        n_tiles = n_groups * group_inner // LANES
        quarters = end_ref.shape[0] // n_tiles
        depth = n_state // quarters
        for t in range(n_tiles):
            for q in range(quarters):
                end_ref[t * quarters + q, 0:depth] = state[q * depth:(q + 1) * depth, t * LANES:(t + 1) * LANES]
                end_ref[t * quarters + q, depth:depth + PIECE_PAD] = decay[:, t * LANES:(t + 1) * LANES]


def exchange_kernel(sp_size, depth, end_ref, in_ref, gathered, starts, recv, send_sem, recv_sem, send_sem2, recv_sem2):
    me = lax.axis_index("sp")
    barrier = pltpu.get_barrier_semaphore()

    def greet(k, carry):
        peer = lax.rem(me + k, sp_size)
        pl.semaphore_signal(barrier, inc=1, device_id={"sp": peer}, device_id_type=pl.DeviceIdType.MESH)
        return carry

    lax.fori_loop(1, sp_size, greet, 0)
    pl.semaphore_wait(barrier, sp_size - 1)

    def send_out(k, carry):
        peer = lax.rem(me + k, sp_size)
        pltpu.make_async_remote_copy(
            src_ref=end_ref.at[peer], dst_ref=gathered.at[me], send_sem=send_sem, recv_sem=recv_sem,
            device_id={"sp": peer}, device_id_type=pl.DeviceIdType.MESH).start()
        return carry

    lax.fori_loop(1, sp_size, send_out, 0)
    others = pl.ds(0, sp_size - 1)
    all_out = pltpu.make_async_copy(end_ref.at[others], gathered.at[others], recv_sem)
    all_out.wait()
    pltpu.make_async_copy(end_ref.at[others], gathered.at[others], send_sem).wait()
    gathered[me] = end_ref[me]

    def scan_step(j, carry):
        starts[j] = carry
        return gathered[j, depth:depth + 1] * carry + gathered[j, 0:depth]

    lax.fori_loop(0, sp_size, scan_step, jnp.zeros((depth, LANES), F32))

    def send_back(k, carry):
        peer = lax.rem(me + k, sp_size)
        pltpu.make_async_remote_copy(
            src_ref=starts.at[peer], dst_ref=recv.at[me], send_sem=send_sem2, recv_sem=recv_sem2,
            device_id={"sp": peer}, device_id_type=pl.DeviceIdType.MESH).start()
        return carry

    lax.fori_loop(1, sp_size, send_back, 0)
    pltpu.make_async_copy(starts.at[others], recv.at[others], recv_sem2).wait()
    pltpu.make_async_copy(starts.at[others], recv.at[others], send_sem2).wait()
    recv[me] = starts[me]
    in_ref[...] = recv[...]


def ssd_kernel(dims, tp_ref, act_ref, z_ref, dts_ref, in_ref, hp_ref, oh_ref, ch_ref, o_ref, state):
    n_groups, group_inner, n_state, head_rep, half_segs, n_segs = dims
    conv_cols = group_inner + 2 * n_state
    n_heads = n_groups * head_rep
    seg_idx = pl.program_id(0)

    @pl.when(seg_idx == 0)
    def _():
        n_tiles = n_groups * group_inner // LANES
        quarters = in_ref.shape[0] // n_tiles
        depth = n_state // quarters
        for t in range(n_tiles):
            for q in range(quarters):
                state[q * depth:(q + 1) * depth, t * LANES:(t + 1) * LANES] = in_ref[t * quarters + q]

    dt_step = dts_ref[0]
    cum = dts_ref[1]
    seg_total = cum[SEG - 1:SEG]
    end_w = spread(jnp.exp2(seg_total - cum) * dt_step, oh_ref[...])
    from_start = spread(jnp.exp2(cum), oh_ref[...])
    seg_decay = from_start[SEG - 1:SEG]
    lane = lax.broadcasted_iota(jnp.int32, (SEG, LANES), 1)
    flipped = jnp.where(lane < n_heads, cum, dt_step).T
    row_id = lax.broadcasted_iota(jnp.int32, (SEG, SEG), 0)
    causal = row_id >= lane
    first_half = lane < LANES // 2

    for g in range(n_groups):
        c0 = g * conv_cols
        i0, i1 = g * group_inner, (g + 1) * group_inner
        x_mat = act_ref[:, c0:c0 + group_inner]
        b_mat = act_ref[:, c0 + group_inner:c0 + group_inner + n_state]
        c_mat = act_ref[:, c0 + group_inner + n_state:c0 + conv_cols]
        c_dot_b = lax.dot_general(c_mat, b_mat, (((1,), (1,)), ((), ())), preferred_element_type=F32)
        diag = []
        for pair in range(head_rep // 2):
            scores = []
            for h in (g * head_rep + 2 * pair, g * head_rep + 2 * pair + 1):
                gap = cum[:, h:h + 1] - flipped[h:h + 1]
                weights = jnp.where(causal, jnp.exp2(gap), 0.0)
                scores.append((c_dot_b * weights * flipped[n_heads + h:n_heads + h + 1]).astype(BF16))
            x_pair = x_mat[:, pair * LANES:(pair + 1) * LANES]
            zero = jnp.zeros_like(x_pair)
            x_both = jnp.concatenate([jnp.where(first_half, x_pair, zero), jnp.where(first_half, zero, x_pair)], axis=0)
            diag.append(jnp.dot(jnp.concatenate(scores, axis=1), x_both, preferred_element_type=F32))
        y_diag = jnp.concatenate(diag, axis=1)
        held = state[:, i0:i1]
        y_off = jnp.dot(c_mat, held.astype(BF16), preferred_element_type=F32) * from_start[:, i0:i1]
        x_wide = x_mat.astype(F32)
        y_ssd = y_diag + y_off + ch_ref[0:1, i0:i1] * x_wide
        weighted = (x_wide * end_w[:, i0:i1]).astype(BF16)
        new = lax.dot_general(b_mat, weighted, (((0,), (0,)), ((), ())), preferred_element_type=F32)
        state[:, i0:i1] = held * seg_decay[:, i0:i1] + new
        gate = z_ref[:, i0:i1].astype(F32)
        gated = y_ssd * (gate / (1.0 + jnp.exp(-gate)))
        inv_rms = lax.rsqrt(jnp.mean(gated * gated, axis=-1, keepdims=True) + NORM_EPS)
        o_ref[0, :, i0:i1] = (gated * inv_rms * ch_ref[1:2, i0:i1]).astype(BF16)


def solution(mesh):
    sp_size, tp_size = mesh.shape["sp"], mesh.shape["tp"]
    row_spec = P(("dp", "sp", "tp"), None)
    swap = [(0, 1), (1, 0)]

    def layer_block(tokens, w_in, conv_w, conv_bias, a_log, dt_bias, d_skip, norm_w, w_out):
        n_groups, conv_cols = conv_bias.shape
        n_heads = a_log.shape[0]
        inner_dim = norm_w.shape[0]
        head_rep = n_heads // n_groups
        group_inner = inner_dim // n_groups
        head_dim = inner_dim // n_heads
        n_state = (conv_cols - group_inner) // 2
        half = tokens.shape[0]
        half_segs = half // SEG
        n_segs = 2 * half_segs
        dims = (n_groups, group_inner, n_state, head_rep, half_segs, n_segs)
        all_cols = w_in.shape[1]
        tp_idx = lax.axis_index("tp")
        tp_arr = tp_idx.reshape(1).astype(jnp.int32)

        other = lax.ppermute(tokens, "tp", swap)
        proj_own = jnp.dot(tokens, w_in, preferred_element_type=F32).astype(BF16)
        proj_oth = jnp.dot(other, w_in, preferred_element_type=F32).astype(BF16)
        tail = jnp.where(tp_idx == 1, proj_own[half - 8:], proj_oth[half - 8:])
        halo = lax.ppermute(tail, "sp", [(i, i + 1) for i in range(sp_size - 1)])

        head_par = jnp.concatenate([jnp.tile(a_log, 4)[None], jnp.tile(dt_bias, 4)[None]], axis=0)
        chan_par = jnp.stack([jnp.repeat(d_skip, head_dim), norm_w.astype(F32)])
        head_of = jnp.arange(inner_dim) // head_dim
        lane_head = jnp.where(jnp.arange(LANES) < 3 * n_heads, jnp.arange(LANES) % n_heads, -1)
        one_hot = (lane_head[:, None] == head_of[None, :]).astype(BF16)

        n_pieces = sp_size
        depth = n_state * inner_dim // LANES // n_pieces
        conv = pl.pallas_call(
            functools.partial(conv_kernel, dims),
            grid_spec=pltpu.PrefetchScalarGridSpec(
                num_scalar_prefetch=1, grid=(n_segs,),
                in_specs=[
                    pl.BlockSpec((SEG, all_cols), lambda i, tp: (jnp.where(i // half_segs == tp[0], i % half_segs, half_segs - 1), 0)),
                    pl.BlockSpec((SEG, all_cols), lambda i, tp: (jnp.where(i // half_segs == tp[0], half_segs - 1, i % half_segs), 0)),
                    pl.BlockSpec((8, all_cols), lambda i, tp: (0, 0)),
                    pl.BlockSpec((4, n_groups * conv_cols), lambda i, tp: (0, 0)),
                    pl.BlockSpec((1, n_groups * conv_cols), lambda i, tp: (0, 0)),
                    pl.BlockSpec((2, LANES), lambda i, tp: (0, 0)),
                    pl.BlockSpec((LANES, inner_dim), lambda i, tp: (0, 0)),
                ],
                out_specs=[
                    pl.BlockSpec((SEG, inner_dim), lambda i, tp: (i, 0)),
                    pl.BlockSpec((SEG, n_groups * conv_cols), lambda i, tp: (i, 0)),
                    pl.BlockSpec((2, SEG, LANES), lambda i, tp: (0, i, 0)),
                    pl.BlockSpec((n_pieces, depth + PIECE_PAD, LANES), lambda i, tp: (0, 0, 0)),
                ],
                scratch_shapes=[
                    pltpu.VMEM((n_groups, SEG + 8, conv_cols), F32),
                    pltpu.VMEM((n_state, inner_dim), F32),
                    pltpu.VMEM((1, LANES), F32),
                ]),
            out_shape=[
                jax.ShapeDtypeStruct((2 * half, inner_dim), BF16),
                jax.ShapeDtypeStruct((2 * half, n_groups * conv_cols), BF16),
                jax.ShapeDtypeStruct((2, 2 * half, LANES), F32),
                jax.ShapeDtypeStruct((n_pieces, depth + PIECE_PAD, LANES), F32),
            ],
            compiler_params=pltpu.CompilerParams(vmem_limit_bytes=48 * 2**20),
            name="conv_states",
        )
        gate_z, act, dts, end_state = conv(
            tp_arr, proj_own, proj_oth, halo, conv_w.reshape(4, n_groups * conv_cols).astype(F32),
            conv_bias.reshape(1, n_groups * conv_cols).astype(F32), head_par, one_hot)

        incoming = pl.pallas_call(
            functools.partial(exchange_kernel, sp_size, depth),
            out_shape=jax.ShapeDtypeStruct((n_pieces, depth, LANES), F32),
            in_specs=[pl.BlockSpec(memory_space=pltpu.VMEM)],
            out_specs=pl.BlockSpec(memory_space=pltpu.VMEM),
            scratch_shapes=[
                pltpu.VMEM((n_pieces, depth + PIECE_PAD, LANES), F32),
                pltpu.VMEM((n_pieces, depth, LANES), F32),
                pltpu.VMEM((n_pieces, depth, LANES), F32),
                pltpu.SemaphoreType.DMA, pltpu.SemaphoreType.DMA,
                pltpu.SemaphoreType.DMA, pltpu.SemaphoreType.DMA,
            ],
            compiler_params=pltpu.CompilerParams(collective_id=0, has_side_effects=True),
            name="state_exchange",
        )(end_state)

        out_rows = pl.pallas_call(
            functools.partial(ssd_kernel, dims),
            grid_spec=pltpu.PrefetchScalarGridSpec(
                num_scalar_prefetch=1, grid=(n_segs,),
                in_specs=[
                    pl.BlockSpec((SEG, n_groups * conv_cols), lambda i, tp: (i, 0)),
                    pl.BlockSpec((SEG, inner_dim), lambda i, tp: (i, 0)),
                    pl.BlockSpec((2, SEG, LANES), lambda i, tp: (0, i, 0)),
                    pl.BlockSpec((n_pieces, depth, LANES), lambda i, tp: (0, 0, 0)),
                    pl.BlockSpec((2, LANES), lambda i, tp: (0, 0)),
                    pl.BlockSpec((LANES, inner_dim), lambda i, tp: (0, 0)),
                    pl.BlockSpec((2, inner_dim), lambda i, tp: (0, 0)),
                ],
                out_specs=pl.BlockSpec((1, SEG, inner_dim), lambda i, tp: (jnp.where(i // half_segs == tp[0], 0, 1), i % half_segs, 0)),
                scratch_shapes=[pltpu.VMEM((n_state, inner_dim), F32)]),
            out_shape=jax.ShapeDtypeStruct((2, half, inner_dim), BF16),
            compiler_params=pltpu.CompilerParams(vmem_limit_bytes=48 * 2**20),
            name="ssd_gate_norm",
        )(tp_arr, act, gate_z, dts, incoming, head_par, one_hot, chan_par)

        part_oth = jnp.dot(out_rows[1], w_out, preferred_element_type=F32).astype(BF16)
        received = lax.ppermute(part_oth, "tp", swap)
        part_own = lax.reduce_precision(jnp.dot(out_rows[0], w_out, preferred_element_type=F32), 8, 7)
        return (tokens.astype(F32) + part_own + received.astype(F32)).astype(BF16)

    return jax.shard_map(
        layer_block,
        mesh=mesh,
        in_specs=(row_spec, P(None, "tp"), P(None, "tp", None), P("tp", None), P("tp"), P("tp"), P("tp"), P("tp"), P("tp", None)),
        out_specs=row_spec,
        check_vma=False)
```

time: 2200 us -> 263 us (0.12)
  waiting for transfers between devices: 1300 us -> 10.2 us
  starting transfers between devices: 443 us -> 6.14 us
  local copies, waits for them, and re-layouts: 163 us -> 4.61 us
  Pallas kernels: 0 us -> 127 us
  other arithmetic: 109 us -> 2.33 us
  matrix products: 158 us -> 113 us
    ppermute x64 -> x3, waiting for transfers between devices: 1120 us -> 10.2 us  [the longest x1 8.66 us: layer_block(): received = lax.ppermute(part_oth, 'tp', swap)]
    ppermute x64 -> x3, starting transfers between devices: 443 us -> 6.14 us  [the longest x1 3.45 us: layer_block(): halo = lax.ppermute(tail, 'sp', [(i, i + 1) for i in range(sp_size - 1)])]
    reduce_scatter x1 -> x0, waiting for transfers between devices: 154 us -> none  [layer_block(): lax.psum_scatter(partial_out, 'tp', scatter_dimension=0, tiled=True)]
    pallas_call x0 -> x3, Pallas kernels: none -> 127 us  [the longest x1 47.1 us: layer_block(): pl.pallas_call(functools.partial(exchange_kernel, sp_size, depth), out_sh...]
    reshape x4 -> x0, local copies, waits for them, and re-layouts: 51 us -> none  [the longest x2 50.8 us: layer_block(): (y_diag + y_off).reshape(seq_blk, n_groups, head_rep, head_dim)]
    convert_element_type x6 -> x1, other arithmetic: 49.7 us -> 0.15 us  [layer_block(): one_hot = (lane_head[:, None] == head_of[None, :]).astype(BF16)]
    dot_general x8 -> x4, matrix products: 158 us -> 113 us  [the longest x1 40.4 us: layer_block(): proj_oth = jnp.dot(other, w_in, preferred_element_type=F32).astype(BF16)]
    unnamed x29 -> x12, local copies, waits for them, and re-layouts: 44.3 us -> 2.31 us
  transfers between devices with their start and end apart: 66 -> 3, of which waited for: 65 -> 2; matrix products, arithmetic and copies ran while one was open for 3% -> 16% of each run, Pallas kernels for 0% -> 0%
where the time goes in v1:
time: 263 us
  Pallas kernels  127 us (48%)
  matrix products  113 us (43%)
  waiting for transfers between devices  10.2 us (4%)
  starting transfers between devices  6.14 us (2%)
  local copies, waits for them, and re-layouts  4.61 us (2%)
    pallas_call x1, Pallas kernels, layer_block(): pl.pallas_call(functools.partial(exchange_kernel, sp_size, depth), out_sh...  47.1 us
    pallas_call x1, Pallas kernels, layer_block(): conv(tp_arr, proj_own, proj_oth, halo, conv_w.reshape(4, n_groups * conv_...  44.3 us
    dot_general x1, matrix products, layer_block(): proj_oth = jnp.dot(other, w_in, preferred_element_type=F32).astype(BF16)  40.4 us
    dot_general x1, matrix products, layer_block(): proj_own = jnp.dot(tokens, w_in, preferred_element_type=F32).astype(BF16)  36.6 us
    pallas_call x1, Pallas kernels, layer_block(): pl.pallas_call(functools.partial(ssd_kernel, dims), grid_spec=pltpu.Prefe...  35.5 us
    dot_general x1, matrix products, layer_block(): jnp.dot(out_rows[0], w_out, preferred_element_type=F32)  18.8 us
    dot_general x1, matrix products, layer_block(): jnp.dot(out_rows[1], w_out, preferred_element_type=F32).astype(BF16)  17 us
    ppermute x1, waiting for transfers between devices, layer_block(): received = lax.ppermute(part_oth, 'tp', swap)  8.66 us
  transfers between devices with their start and end apart: 3, of which 2 were waited for; matrix products, arithmetic and copies ran while one was open for 16% of the time, Pallas kernels for 0%

profile of v1, /device:TPU:1, one launch (start us, length us, event | category | flops | bytes accessed | tf_op | source)
XLA Modules:
  0.0 263.0 jit_solution(8733680643937000357)
XLA Ops:
  0.0 1.4 collective-permute-start
  1.4 0.7 tile.4
  2.0 0.1 broadcast_in_dim_tile.6
  2.1 0.7 tile.5
  2.8 0.1 broadcast_in_dim_tile.7
  2.9 0.7 convert_bitcast_fusion
  3.6 0.7 convert_bitcast_fusion.1
  4.3 0.7 broadcast_in_dim.10
  5.1 0.1 stack_reshape.3
  5.1 0.7 stack.12
  5.8 0.1 compare_convert_fusion.oh_ref
  6.0 36.6 %convolution_convert_fusion.1.own_ref = bf16[1024,5152]{1,0:T(8,128)(2,1)S(1)} fusion(bf16[1024,2688]{1,0:T(8,128)(2,1)} %param.9, bf16[2688,5152]{0,1:T(8,128)(2,1)} %param.10), kind=kOutput, calls=%fused_computation.1 | convolution fusion | flops 28367159296 | bytes 43753472 | tf_op jit(solution)/shard_map/dot_general | solution.py:221
  42.6 0.0 copy-start.2
  42.6 0.0 collective-permute-done
  42.6 40.4 %convolution_convert_fusion.oth_ref = bf16[1024,5152]{1,0:T(8,128)(2,1)S(1)} fusion(bf16[1024,2688]{1,0:T(8,128)(2,1)} %collective-permute-done, bf16[2688,5152]{0,1:T(8,128)(2,1)} %param.10), kind=kOutput, calls=%fused_computation | convolution fusion | flops 28367159296 | bytes 43753472 | tf_op jit(solution)/shard_map/dot_general | solution.py:222
  83.0 0.0 copy-done.2
  83.0 0.0 copy-start.3
  83.1 3.4 %collective-permute-start.1 = (bf16[8,5152]{1,0:T(8,128)(2,1)S(1)}, bf16[8,5152]{1,0:T(8,128)(2,1)S(1)}, u32[]{:S(2)}, u32[]{:S(2)}) collective-permute-start(bf16[8,5152]{1,0:T(8,128)(2,1)S(1)} %slice_select_fusion), channel_id=1, source_target_pairs={{0,2},{2,4},{4,6},{6,8},{8,10},{10,12},{12,14},{14,16},{16,18},{18... | collective-permute-start | bytes 247304 | tf_op jit(solution)/shard_map/ppermute | solution.py:224
  86.5 1.6 collective-permute-done.1.halo_ref
  88.1 0.0 copy-done.3
  88.1 44.3 %conv_states.1 = (bf16[2048,2048]{1,0:T(8,128)(2,1)}, bf16[2048,3072]{1,0:T(8,128)(2,1)}, f32[2,2048,128]{2,1,0:T(8,128)S(1)}, f32[64,40,128]{2,1,0:T(8,128)S(1)}) custom-call(s32[1]{0:T(128)} %bitcast.tp_ref, bf16[1024,5152]{1,0:T(8,128)(2,1)} %copy-done.2, bf16[1024,5152]{1,0:T(8,128)(2,1)} %copy-done.3, ...), custom_call_target="tpu_custom_call" | custom-call | tf_op jit(solution)/shard_map/conv_states/pallas_call | solution.py:267
  132.4 1.1 copy-done.1
  133.5 47.1 %state_exchange.1.in_ref = f32[64,32,128]{2,1,0:T(8,128)} custom-call(f32[64,40,128]{2,1,0:T(8,128)} %copy-done.1), custom_call_target="tpu_custom_call" | custom-call | tf_op jit(solution)/shard_map/state_exchange/pallas_call | solution.py:271
  180.6 0.0 copy-start
  180.6 1.2 copy-done
  181.8 35.5 %ssd_gate_norm.1 = bf16[2,1024,2048]{2,1,0:T(8,128)(2,1)} custom-call(s32[1]{0:T(128)} %bitcast.tp_ref, bf16[2048,3072]{1,0:T(8,128)(2,1)} %get-tuple-element.9.act_ref, bf16[2048,2048]{1,0:T(8,128)(2,1)} %get-tuple-element.10.z_ref, f32[2,2048,128]{2,1,0:T(8,128)S(1)} %get-tuple-element.11.dts_ref, f32[64,32,128]{2,1,0:T(8,128)S(1)} %copy-done, ...), custom_call_target="tpu_custom_call" | custom-call | tf_op jit(solution)/shard_map/ssd_gate_norm/pallas_call | solution.py:287
  217.2 0.0 copy-start.4
  217.3 17.0 %convolution_convert_fusion.2 = bf16[1024,2688]{1,0:T(8,128)(2,1)S(1)} fusion(bf16[2048,2688]{1,0:T(8,128)(2,1)} %param.17, bf16[2,1024,2048]{2,1,0:T(8,128)(2,1)} %ssd_gate_norm.1), kind=kOutput, calls=%fused_computation.3 | convolution fusion | flops 11277041664 | bytes 20709376 | tf_op jit(solution)/shard_map/dot_general | solution.py:307
  234.2 1.3 collective-permute-start.2
  235.6 8.7 %collective-permute-done.2 = bf16[1024,2688]{1,0:T(8,128)(2,1)S(1)} collective-permute-done((bf16[1024,2688]{1,0:T(8,128)(2,1)S(1)}, bf16[1024,2688]{1,0:T(8,128)(2,1)S(1)}, u32[]{:S(2)}, u32[]{:S(2)}) %collective-permute-start.2) | collective-permute-done | bytes 5505056 | tf_op jit(solution)/shard_map/ppermute | solution.py:308
  244.2 0.0 copy-done.4
  244.2 18.8 %add_convert_fusion = bf16[1024,2688]{1,0:T(8,128)(2,1)} fusion(bf16[1024,2688]{1,0:T(8,128)(2,1)S(1)} %collective-permute-done.2, bf16[1024,2688]{1,0:T(8,128)(2,1)} %param.9, bf16[2048,2688]{1,0:T(8,128)(2,1)} %param.17, bf16[2,1024,2048]{2,1,0:T(8,128)(2,1)S(1)} %copy-done.4), kind=kOutput, calls=%fused_computation.2 | convolution fusion | flops 11290804224 | bytes 31719424 | tf_op jit(solution)/shard_map/dot_general | solution.py:309
  (8 shorter events, 0.1 us)
Async XLA Ops:
  0.0 42.6 %collective-permute-start = (bf16[1024,2688]{1,0:T(8,128)(2,1)}, bf16[1024,2688]{1,0:T(8,128)(2,1)}, u32[]{:S(2)}, u32[]{:S(2)}) collective-permute-start(bf16[1024,2688]{1,0:T(8,128)(2,1)} %param.9), channel_id=1, source_target_pairs={{0,1},{1,0},{2,3},{3,2},{4,5},{5,4},{6,7},{7,6},{8,9},{9,8},{10,11... | collective-permute-start | bytes 16515080 | tf_op jit(solution)/shard_map/ppermute | solution.py:220
  42.6 40.4 %copy-start.2 = (bf16[1024,5152]{1,0:T(8,128)(2,1)}, bf16[1024,5152]{1,0:T(8,128)(2,1)S(1)}, u32[]{:S(2)}) copy-start(bf16[1024,5152]{1,0:T(8,128)(2,1)S(1)} %convolution_convert_fusion.1.own_ref) | copy-start | bytes 31653892
  83.0 5.1 %copy-start.3 = (bf16[1024,5152]{1,0:T(8,128)(2,1)}, bf16[1024,5152]{1,0:T(8,128)(2,1)S(1)}, u32[]{:S(2)}) copy-start(bf16[1024,5152]{1,0:T(8,128)(2,1)S(1)} %convolution_convert_fusion.oth_ref) | copy-start | bytes 31653892
  83.1 5.0 %collective-permute-start.1 = (bf16[8,5152]{1,0:T(8,128)(2,1)S(1)}, bf16[8,5152]{1,0:T(8,128)(2,1)S(1)}, u32[]{:S(2)}, u32[]{:S(2)}) collective-permute-start(bf16[8,5152]{1,0:T(8,128)(2,1)S(1)} %slice_select_fusion), channel_id=1, source_target_pairs={{0,2},{2,4},{4,6},{6,8},{8,10},{10,12},{12,14},{14,16},{16,18},{18... | collective-permute-start | bytes 247304 | tf_op jit(solution)/shard_map/ppermute | solution.py:224
  132.4 1.1 copy-start.1
  180.6 1.2 copy-start
  217.2 27.0 %copy-start.4 = (bf16[2,1024,2048]{2,1,0:T(8,128)(2,1)S(1)}, bf16[2,1024,2048]{2,1,0:T(8,128)(2,1)}, u32[]{:S(2)}) copy-start(bf16[2,1024,2048]{2,1,0:T(8,128)(2,1)} %ssd_gate_norm.1) | copy-start | bytes 25165828
  234.2 10.0 %collective-permute-start.2 = (bf16[1024,2688]{1,0:T(8,128)(2,1)S(1)}, bf16[1024,2688]{1,0:T(8,128)(2,1)S(1)}, u32[]{:S(2)}, u32[]{:S(2)}) collective-permute-start(bf16[1024,2688]{1,0:T(8,128)(2,1)S(1)} %convolution_convert_fusion.2), channel_id=1, source_target_pairs={{0,1},{1,0},{2,3},{3,2},{4,5},{5,4},{6,7},{7,6},{8,9},{9,8},{10,11... | collective-permute-start | bytes 16515080 | tf_op jit(solution)/shard_map/ppermute | solution.py:308

commit v2 on v0

v2 whole, which is shorter than its diff:
```python
import functools

import jax
import jax.numpy as jnp
from jax import lax
from jax.experimental import pallas as pl
from jax.experimental.pallas import tpu as pltpu
from jax.sharding import PartitionSpec as P

SEG = 128
SUB = 256
HALO = 16
NORM_EPS = 1e-5
LANES = 128
PIECE_PAD = 8
LOG2E = 1.4426950408889634
F32 = jnp.float32
BF16 = jnp.bfloat16


def spread(values, one_hot):
    n_heads = LANES // 4
    high = values.astype(BF16)
    rest = values - high.astype(F32)
    mid = rest.astype(BF16)
    low = (rest - mid.astype(F32)).astype(BF16)
    lane = lax.broadcasted_iota(jnp.int32, values.shape, 1)
    parts = jnp.where(lane < n_heads, high.astype(F32), jnp.where(lane < 2 * n_heads, mid.astype(F32), low.astype(F32)))
    parts = jnp.where(lane < 3 * n_heads, parts, 0.0).astype(BF16)
    return jnp.dot(parts, one_hot, preferred_element_type=F32)


CONTRACT_LAST = (((1,), (1,)), ((), ()))


def weight_copy(wt_ref, weights, sems, group_id, group_cols, offset):
    rows = weights.shape[1]
    lo = pl.multiple_of(group_id * group_cols + offset, 8)
    slot = lax.rem(group_id, 2)
    return pltpu.make_async_copy(wt_ref.at[pl.ds(lo, rows)], weights.at[slot], sems.at[slot])


def project_conv_kernel(dims, tp_ref, own_ref, oth_ref, halo_ref, wt_ref,
                        cw_ref, cb_ref, hp_ref, oh_ref, act_ref, dts_ref, end_ref,
                        x_buf, weights, w_dt, ext0, ext1, ext2, ext3, state, total, sems, wsems, dsems):
    n_groups, group_inner, n_state, head_rep, half = dims
    group_id, half_id = pl.program_id(0), pl.program_id(1)
    n_heads = n_groups * head_rep
    exts = (ext0, ext1, ext2, ext3)

    def copies(first, second):
        return [
            lambda: pltpu.make_async_copy(halo_ref, x_buf.at[0, pl.ds(0, HALO)], sems.at[0]),
            lambda: pltpu.make_async_copy(first, x_buf.at[0, pl.ds(HALO, half)], sems.at[1]),
            lambda: pltpu.make_async_copy(first.at[pl.ds(half - HALO, HALO)], x_buf.at[1, pl.ds(0, HALO)], sems.at[2]),
            lambda: pltpu.make_async_copy(second, x_buf.at[1, pl.ds(HALO, half)], sems.at[3]),
        ]

    start = (group_id == 0) & (half_id == 0)

    @pl.when(start & (tp_ref[0] == 0))
    def _():
        for c in copies(own_ref, oth_ref):
            c().start()

    @pl.when(start & (tp_ref[0] == 1))
    def _():
        for c in copies(oth_ref, own_ref):
            c().start()

    group_cols = 2 * group_inner + 2 * n_state + head_rep
    dt_copies = [
        pltpu.make_async_copy(wt_ref.at[pl.ds((g + 1) * group_cols - head_rep, head_rep)], w_dt.at[pl.ds(g * head_rep, head_rep)], dsems.at[g])
        for g in range(n_groups)]

    @pl.when(start)
    def _():
        weight_copy(wt_ref, weights, wsems, group_id, group_cols, group_inner).start()
        w_dt[n_heads:LANES] = jnp.zeros((LANES - n_heads, w_dt.shape[1]), BF16)
        for c in dt_copies:
            c.start()
        total[...] = jnp.zeros_like(total)
        for c in dt_copies:
            c.wait()
        for c in copies(own_ref, oth_ref)[:2]:
            c().wait()

    @pl.when((group_id == 0) & (half_id == 1))
    def _():
        for c in copies(own_ref, oth_ref)[2:]:
            c().wait()

    @pl.when(half_id == 0)
    def _():
        weight_copy(wt_ref, weights, wsems, group_id, group_cols, group_inner).wait()
        state[...] = jnp.zeros_like(state)

    @pl.when((half_id == 0) & (group_id < n_groups - 1))
    def _():
        weight_copy(wt_ref, weights, wsems, group_id + 1, group_cols, group_inner).start()

    w_slot = lax.rem(group_id, 2)

    row0 = half_id * half

    @pl.when(group_id == 0)
    def _():
        def step(s, carry):
            at = pl.ds(pl.multiple_of(HALO + s * SUB, 16), SUB)
            raw = lax.dot_general(x_buf[half_id, at, :], w_dt[...], CONTRACT_LAST, preferred_element_type=F32).astype(BF16).astype(F32)
            raw = raw + pltpu.roll(raw, n_heads, 1) + pltpu.roll(raw, 2 * n_heads, 1) + pltpu.roll(raw, 3 * n_heads, 1)
            dt_step = jax.nn.softplus(raw + hp_ref[1:2])
            log_decay = -jnp.exp(hp_ref[0:1]) * dt_step * LOG2E
            row_id = lax.broadcasted_iota(jnp.int32, (SEG, SEG), 0)
            col_id = lax.broadcasted_iota(jnp.int32, (SEG, SEG), 1)
            tri = (row_id >= col_id).astype(F32)
            for q in range(SUB // SEG):
                lo, hi = q * SEG, (q + 1) * SEG
                cum = jnp.dot(tri, log_decay[lo:hi], precision=lax.Precision.HIGHEST, preferred_element_type=F32)
                out = pl.ds(pl.multiple_of(row0 + s * SUB + lo, SEG), SEG)
                dts_ref[0, out, :] = dt_step[lo:hi]
                dts_ref[1, out, :] = cum
                dts_ref[2, out, :] = cum + total[...]
                total[...] += cum[SEG - 1:SEG]
            return carry
        lax.fori_loop(0, half // SUB, step, 0)

    n_cols = weights.shape[1] // LANES

    def matmul(s):
        lo = 0 if s == 0 else HALO
        rows = x_buf[half_id, s * SUB + lo:HALO + (s + 1) * SUB, :]
        raw = lax.dot_general(rows, weights[w_slot], CONTRACT_LAST, preferred_element_type=F32).astype(BF16).astype(F32)
        for t in range(n_cols):
            exts[s][t, lo:HALO + SUB] = raw[:, t * LANES:(t + 1) * LANES]

    def convolved(s, t):
        ext = exts[s]
        if s > 0:
            ext[t, 8:HALO] = exts[s - 1][t, HALO + SUB - 8:HALO + SUB]
        lanes = slice(t * LANES, (t + 1) * LANES)
        acc = cb_ref[:, lanes] + ext[t, HALO - 3:HALO - 3 + SUB] * cw_ref[0:1, lanes]
        for k in range(1, 4):
            acc = acc + ext[t, HALO - 3 + k:HALO - 3 + k + SUB] * cw_ref[k:k + 1, lanes]
        act = (acc / (1.0 + jnp.exp(-acc))).astype(BF16)
        act_ref[s * SUB:(s + 1) * SUB, lanes] = act
        return act

    def vector(s):
        n_x = group_inner // LANES
        b_all = convolved(s, n_x)
        convolved(s, n_x + 1)
        at = pl.ds(pl.multiple_of(row0 + s * SUB, SUB), SUB)
        dt_step, cum = dts_ref[0, at, :], dts_ref[1, at, :]
        ends = [cum[(q + 1) * SEG - 1:(q + 1) * SEG] for q in range(SUB // SEG)]
        last = jnp.concatenate([jnp.broadcast_to(e, (SEG, LANES)) for e in ends], axis=0)
        end_w = spread(jnp.exp2(last - cum) * dt_step, oh_ref[...])
        decay = spread(jnp.exp2(jnp.concatenate([jnp.broadcast_to(e, (8, LANES)) for e in ends], axis=0)), oh_ref[...])
        weighted = [(convolved(s, t).astype(F32) * end_w[:, t * LANES:(t + 1) * LANES]).astype(BF16) for t in range(n_x)]
        weighted = jnp.concatenate(weighted, axis=1)
        for q in range(SUB // SEG):
            lo, hi = q * SEG, (q + 1) * SEG
            new = lax.dot_general(b_all[lo:hi], weighted[lo:hi], (((0,), (0,)), ((), ())), preferred_element_type=F32)
            state[...] = state[...] * decay[8 * q:8 * q + 1] + new

    matmul(0)
    for s in range(1, half // SUB):
        matmul(s)
        vector(s - 1)
    vector(half // SUB - 1)

    @pl.when(half_id == 1)
    def _():
        decay = spread(jnp.exp2(jnp.broadcast_to(total[...], (8, LANES))), oh_ref[...])
        n_tiles = group_inner // LANES
        quarters = end_ref.shape[0] // (n_groups * n_tiles)
        depth = n_state // quarters
        for t in range(n_tiles):
            for q in range(quarters):
                piece = (group_id * n_tiles + t) * quarters + q
                end_ref[piece, 0:depth] = state[q * depth:(q + 1) * depth, t * LANES:(t + 1) * LANES]
                end_ref[piece, depth:depth + PIECE_PAD] = decay[:, t * LANES:(t + 1) * LANES]


def gate_ssd_kernel(dims, sp_size, end_ref, own_ref, oth_ref, wt_ref, act_ref, dts_ref, oh_ref, ds_ref, z_ref, y_ref, in_ref,
                    x_buf, weights, state, gathered, starts, received, xsems, wsems, send_sem, recv_sem, send_sem2, recv_sem2):
    n_groups, group_inner, n_state, head_rep, half = dims
    conv_cols = group_inner + 2 * n_state
    group_cols = 2 * group_inner + 2 * n_state + head_rep
    n_heads = n_groups * head_rep
    depth = starts.shape[1]
    step_id = pl.program_id(0)
    n_z = 2 * n_groups
    me = lax.axis_index("sp")
    others = pl.ds(0, sp_size - 1)
    mesh_id = pl.DeviceIdType.MESH

    def x_copy(k):
        return pltpu.make_async_copy((own_ref, oth_ref)[k], x_buf.at[k], xsems.at[k])

    @pl.when(step_id == 0)
    def _():
        weight_copy(wt_ref, weights, wsems, 0, group_cols, 0).start()
        x_copy(0).start()
        x_copy(1).start()
        barrier = pltpu.get_barrier_semaphore()

        def greet(k, carry):
            pl.semaphore_signal(barrier, inc=1, device_id={"sp": lax.rem(me + k, sp_size)}, device_id_type=mesh_id)
            return carry

        lax.fori_loop(1, sp_size, greet, 0)

    @pl.when(step_id == 1)
    def _():
        pl.semaphore_wait(pltpu.get_barrier_semaphore(), sp_size - 1)

        def send_out(k, carry):
            peer = lax.rem(me + k, sp_size)
            pltpu.make_async_remote_copy(
                src_ref=end_ref.at[peer], dst_ref=gathered.at[me], send_sem=send_sem, recv_sem=recv_sem,
                device_id={"sp": peer}, device_id_type=mesh_id).start()
            return carry

        lax.fori_loop(1, sp_size, send_out, 0)

    @pl.when(step_id == n_z)
    def _():
        pltpu.make_async_copy(end_ref.at[others], gathered.at[others], recv_sem).wait()
        pltpu.make_async_copy(end_ref.at[others], gathered.at[others], send_sem).wait()
        gathered[me] = end_ref[me]

        def scan_step(j, carry):
            starts[j] = carry
            return gathered[j, depth:depth + 1] * carry + gathered[j, 0:depth]

        lax.fori_loop(0, sp_size, scan_step, jnp.zeros((depth, LANES), F32))

        def send_back(k, carry):
            peer = lax.rem(me + k, sp_size)
            pltpu.make_async_remote_copy(
                src_ref=starts.at[peer], dst_ref=received.at[me], send_sem=send_sem2, recv_sem=recv_sem2,
                device_id={"sp": peer}, device_id_type=mesh_id).start()
            return carry

        lax.fori_loop(1, sp_size, send_back, 0)
        state[...] = jnp.zeros_like(state)

    @pl.when(step_id < n_z)
    def _():
        group_id, slot = step_id // 2, lax.rem(step_id, 2)

        @pl.when(slot == 0)
        def _():
            weight_copy(wt_ref, weights, wsems, group_id, group_cols, 0).wait()

        @pl.when((slot == 0) & (group_id < n_groups - 1))
        def _():
            weight_copy(wt_ref, weights, wsems, group_id + 1, group_cols, 0).start()

        for k in range(2):
            @pl.when(step_id == k)
            def _(k=k):
                x_copy(k).wait()

        z_ref[0] = lax.dot_general(x_buf[slot], weights[lax.rem(group_id, 2)], CONTRACT_LAST, preferred_element_type=F32).astype(BF16)

    @pl.when(step_id >= n_z)
    def _():
        dt_step = dts_ref[0]
        cum = dts_ref[1]
        seg_total = cum[SEG - 1:SEG]
        end_w = spread(jnp.exp2(seg_total - cum) * dt_step, oh_ref[...])
        from_start = spread(jnp.exp2(cum), oh_ref[...])
        seg_decay = from_start[SEG - 1:SEG]
        lane = lax.broadcasted_iota(jnp.int32, (SEG, LANES), 1)
        flipped = jnp.where(lane < n_heads, cum, dt_step).T
        row_id = lax.broadcasted_iota(jnp.int32, (SEG, SEG), 0)
        causal = row_id >= lane
        first_half = lane < LANES // 2

        for g in range(n_groups):
            c0 = g * conv_cols
            i0, i1 = g * group_inner, (g + 1) * group_inner
            x_mat = act_ref[:, c0:c0 + group_inner]
            b_mat = act_ref[:, c0 + group_inner:c0 + group_inner + n_state]
            c_mat = act_ref[:, c0 + group_inner + n_state:c0 + conv_cols]
            c_dot_b = lax.dot_general(c_mat, b_mat, (((1,), (1,)), ((), ())), preferred_element_type=F32)
            diag = []
            for pair in range(head_rep // 2):
                scores = []
                for h in (g * head_rep + 2 * pair, g * head_rep + 2 * pair + 1):
                    gap = cum[:, h:h + 1] - flipped[h:h + 1]
                    weights = jnp.where(causal, jnp.exp2(gap), 0.0)
                    scores.append((c_dot_b * weights * flipped[n_heads + h:n_heads + h + 1]).astype(BF16))
                x_pair = x_mat[:, pair * LANES:(pair + 1) * LANES]
                zero = jnp.zeros_like(x_pair)
                x_both = jnp.concatenate([jnp.where(first_half, x_pair, zero), jnp.where(first_half, zero, x_pair)], axis=0)
                diag.append(jnp.dot(jnp.concatenate(scores, axis=1), x_both, preferred_element_type=F32))
            y_diag = jnp.concatenate(diag, axis=1)
            held = state[:, i0:i1]
            y_off = jnp.dot(c_mat, held.astype(BF16), preferred_element_type=F32) * from_start[:, i0:i1]
            x_wide = x_mat.astype(F32)
            y_ref[:, i0:i1] = y_diag + y_off + ds_ref[0:1, i0:i1] * x_wide
            weighted = (x_wide * end_w[:, i0:i1]).astype(BF16)
            new = lax.dot_general(b_mat, weighted, (((0,), (0,)), ((), ())), preferred_element_type=F32)
            state[:, i0:i1] = held * seg_decay[:, i0:i1] + new

    @pl.when(step_id == pl.num_programs(0) - 1)
    def _():
        pltpu.make_async_copy(starts.at[others], received.at[others], recv_sem2).wait()
        pltpu.make_async_copy(starts.at[others], received.at[others], send_sem2).wait()
        received[me] = starts[me]
        in_ref[...] = received[...]


def gate_norm_kernel(dims, tp_ref, y_ref, c0_ref, c1_ref, c2_ref, c3_ref, z_ref, dts_ref, in_ref, oh_ref, nw_ref, o_ref, state):
    n_groups, group_inner, n_state, head_rep, half = dims

    @pl.when(pl.program_id(0) == 0)
    def _():
        n_tiles = n_groups * group_inner // LANES
        quarters = in_ref.shape[0] // n_tiles
        depth = n_state // quarters
        for t in range(n_tiles):
            for q in range(quarters):
                state[q * depth:(q + 1) * depth, t * LANES:(t + 1) * LANES] = in_ref[t * quarters + q].astype(BF16)

    from_start = spread(jnp.exp2(dts_ref[0]), oh_ref[...])
    for g, c_ref in enumerate((c0_ref, c1_ref, c2_ref, c3_ref)):
        i0, i1 = g * group_inner, (g + 1) * group_inner
        y_in = jnp.dot(c_ref[...], state[:, i0:i1], preferred_element_type=F32)
        y_ssd = y_ref[:, i0:i1] + y_in * from_start[:, i0:i1]
        gate = z_ref[0, :, i0:i1].astype(F32)
        gated = y_ssd * (gate / (1.0 + jnp.exp(-gate)))
        inv_rms = lax.rsqrt(jnp.mean(gated * gated, axis=-1, keepdims=True) + NORM_EPS)
        o_ref[:, i0:i1] = (gated * inv_rms * nw_ref[0:1, i0:i1].astype(F32)).astype(BF16)


def solution(mesh):
    sp_size, tp_size = mesh.shape["sp"], mesh.shape["tp"]
    row_spec = P(("dp", "sp", "tp"), None)
    swap = [(0, 1), (1, 0)]

    def layer_block(tokens, w_in, conv_w, conv_bias, a_log, dt_bias, d_skip, norm_w, w_out):
        n_groups, conv_cols = conv_bias.shape
        n_heads = a_log.shape[0]
        inner_dim = norm_w.shape[0]
        head_rep = n_heads // n_groups
        group_inner = inner_dim // n_groups
        head_dim = inner_dim // n_heads
        n_state = (conv_cols - group_inner) // 2
        half, width = tokens.shape
        rows = 2 * half
        all_conv = n_groups * conv_cols
        dims = (n_groups, group_inner, n_state, head_rep, half)
        tp_idx = lax.axis_index("tp")
        tp_arr = tp_idx.reshape(1).astype(jnp.int32)
        any_spec = pl.BlockSpec(memory_space=pl.ANY)
        limit = 60 * 2**20
        w_in_t = w_in.T

        other = lax.ppermute(tokens, "tp", swap)
        tail = tokens[half - HALO:]
        edge = [(2 * i + 1, 2 * i + 2) for i in range(sp_size - 1)]
        edge_same = [(2 * i + 1, 2 * i + 3) for i in range(sp_size - 1)]
        halo = lax.ppermute(tail, ("sp", "tp"), edge) + lax.ppermute(tail, ("sp", "tp"), edge_same)

        head_par = jnp.concatenate([jnp.tile(a_log, 4)[None], jnp.tile(dt_bias, 4)[None]], axis=0)
        skip_row = jnp.repeat(d_skip, head_dim)[None]
        head_of = jnp.arange(inner_dim) // head_dim
        lane_head = jnp.where(jnp.arange(LANES) < 3 * n_heads, jnp.arange(LANES) % n_heads, -1)
        one_hot = (lane_head[:, None] == head_of[None, :]).astype(BF16)
        cw = conv_w.reshape(4, all_conv).astype(F32)
        cb = conv_bias.reshape(1, all_conv).astype(F32)

        n_pieces = sp_size
        depth = n_state * inner_dim // LANES // n_pieces
        once = dict(pipeline_mode=pl.Buffered(buffer_count=1))
        act, dts, end_state = pl.pallas_call(
            functools.partial(project_conv_kernel, dims),
            grid_spec=pltpu.PrefetchScalarGridSpec(
                num_scalar_prefetch=1, grid=(n_groups, 2),
                in_specs=[
                    any_spec, any_spec, any_spec, any_spec,
                    pl.BlockSpec((4, conv_cols), lambda g, i, tp: (0, g)),
                    pl.BlockSpec((1, conv_cols), lambda g, i, tp: (0, g)),
                    pl.BlockSpec((2, LANES), lambda g, i, tp: (0, 0)),
                    pl.BlockSpec((LANES, group_inner), lambda g, i, tp: (0, g)),
                ],
                out_specs=[
                    pl.BlockSpec((half, conv_cols), lambda g, i, tp: (i, g)),
                    pl.BlockSpec((3, rows, LANES), lambda g, i, tp: (0, 0, 0), **once),
                    pl.BlockSpec((n_pieces, depth + PIECE_PAD, LANES), lambda g, i, tp: (0, 0, 0), **once),
                ],
                scratch_shapes=[
                    pltpu.VMEM((2, HALO + half, width), BF16),
                    pltpu.VMEM((2, conv_cols, width), BF16),
                    pltpu.VMEM((LANES, width), BF16),
                    pltpu.VMEM((conv_cols // LANES, HALO + SUB, LANES), F32),
                    pltpu.VMEM((conv_cols // LANES, HALO + SUB, LANES), F32),
                    pltpu.VMEM((conv_cols // LANES, HALO + SUB, LANES), F32),
                    pltpu.VMEM((conv_cols // LANES, HALO + SUB, LANES), F32),
                    pltpu.VMEM((n_state, group_inner), F32),
                    pltpu.VMEM((1, LANES), F32),
                    pltpu.SemaphoreType.DMA((4,)),
                    pltpu.SemaphoreType.DMA((2,)),
                    pltpu.SemaphoreType.DMA((n_groups,)),
                ]),
            out_shape=[
                jax.ShapeDtypeStruct((rows, all_conv), BF16),
                jax.ShapeDtypeStruct((3, rows, LANES), F32),
                jax.ShapeDtypeStruct((n_pieces, depth + PIECE_PAD, LANES), F32),
            ],
            compiler_params=pltpu.CompilerParams(vmem_limit_bytes=limit),
            cost_estimate=pl.CostEstimate(flops=2 * rows * width * all_conv, bytes_accessed=2 * width * all_conv, transcendentals=0),
            name="project_conv_states",
        )(tp_arr, tokens, other, halo, w_in_t, cw, cb, head_par, one_hot)

        n_z = 2 * n_groups

        def seg_at(i):
            return jnp.maximum(i - n_z, 0)

        def z_at(i):
            return jnp.minimum(i, n_z - 1)

        gate_z, y_local, incoming = pl.pallas_call(
            functools.partial(gate_ssd_kernel, dims, sp_size),
            grid=(n_z + rows // SEG,),
            in_specs=[
                pl.BlockSpec((n_pieces, depth + PIECE_PAD, LANES), lambda i: (0, 0, 0), **once),
                any_spec, any_spec, any_spec,
                pl.BlockSpec((SEG, all_conv), lambda i: (seg_at(i), 0)),
                pl.BlockSpec((2, SEG, LANES), lambda i: (0, seg_at(i), 0)),
                pl.BlockSpec((LANES, inner_dim), lambda i: (0, 0), **once),
                pl.BlockSpec((1, inner_dim), lambda i: (0, 0)),
            ],
            out_specs=[
                pl.BlockSpec((1, half, group_inner), lambda i: (lax.rem(z_at(i), 2), 0, z_at(i) // 2)),
                pl.BlockSpec((SEG, inner_dim), lambda i: (seg_at(i), 0)),
                pl.BlockSpec((n_pieces, depth, LANES), lambda i: (0, 0, 0), **once),
            ],
            out_shape=[
                jax.ShapeDtypeStruct((2, half, inner_dim), BF16),
                jax.ShapeDtypeStruct((rows, inner_dim), F32),
                jax.ShapeDtypeStruct((n_pieces, depth, LANES), F32),
            ],
            scratch_shapes=[
                pltpu.VMEM((2, half, width), BF16),
                pltpu.VMEM((2, group_inner, width), BF16),
                pltpu.VMEM((n_state, inner_dim), F32),
                pltpu.VMEM((n_pieces, depth + PIECE_PAD, LANES), F32),
                pltpu.VMEM((n_pieces, depth, LANES), F32),
                pltpu.VMEM((n_pieces, depth, LANES), F32),
                pltpu.SemaphoreType.DMA((2,)),
                pltpu.SemaphoreType.DMA((2,)),
                pltpu.SemaphoreType.DMA, pltpu.SemaphoreType.DMA,
                pltpu.SemaphoreType.DMA, pltpu.SemaphoreType.DMA,
            ],
            compiler_params=pltpu.CompilerParams(vmem_limit_bytes=limit, collective_id=0, has_side_effects=True),
            name="gate_ssd_exchange",
        )(end_state, tokens, other, w_in_t, act, dts, one_hot, skip_row)

        def finish(slot):
            def at(i, tp):
                return ((tp[0] + slot) % 2) * (half // SUB) + i

            def c_spec(g):
                return pl.BlockSpec((SUB, LANES), lambda i, tp: (at(i, tp), 6 * g + 5))

            return pl.pallas_call(
                functools.partial(gate_norm_kernel, dims),
                grid_spec=pltpu.PrefetchScalarGridSpec(
                    num_scalar_prefetch=1, grid=(half // SUB,),
                    in_specs=[
                        pl.BlockSpec((SUB, inner_dim), lambda i, tp: (at(i, tp), 0)),
                        c_spec(0), c_spec(1), c_spec(2), c_spec(3),
                        pl.BlockSpec((1, SUB, inner_dim), lambda i, tp: (slot, i, 0)),
                        pl.BlockSpec((1, SUB, LANES), lambda i, tp: (2, at(i, tp), 0)),
                        pl.BlockSpec((n_pieces, depth, LANES), lambda i, tp: (0, 0, 0)),
                        pl.BlockSpec((LANES, inner_dim), lambda i, tp: (0, 0)),
                        pl.BlockSpec((1, inner_dim), lambda i, tp: (0, 0)),
                    ],
                    out_specs=pl.BlockSpec((SUB, inner_dim), lambda i, tp: (i, 0)),
                    scratch_shapes=[pltpu.VMEM((n_state, inner_dim), BF16)]),
                out_shape=jax.ShapeDtypeStruct((half, inner_dim), BF16),
                compiler_params=pltpu.CompilerParams(vmem_limit_bytes=48 * 2**20),
                cost_estimate=pl.CostEstimate(flops=half * width * inner_dim, bytes_accessed=10 * half * inner_dim, transcendentals=0),
                name="gate_norm",
            )(tp_arr, y_local, act, act, act, act, gate_z, dts, incoming, one_hot, norm_w[None])

        rows_oth = finish(1)
        part_oth = jnp.dot(rows_oth, w_out, preferred_element_type=F32).astype(BF16)
        received = lax.ppermute(part_oth, "tp", swap)
        rows_own = finish(0)
        part_own = lax.reduce_precision(jnp.dot(rows_own, w_out, preferred_element_type=F32), 8, 7)
        return (tokens.astype(F32) + part_own + received.astype(F32)).astype(BF16)

    return jax.shard_map(
        layer_block,
        mesh=mesh,
        in_specs=(row_spec, P(None, "tp"), P(None, "tp", None), P("tp", None), P("tp"), P("tp"), P("tp"), P("tp"), P("tp", None)),
        out_specs=row_spec,
        check_vma=False)
```

time: 2200 us -> 211 us (0.10)
  waiting for transfers between devices: 1300 us -> 0.01 us
  starting transfers between devices: 443 us -> 5.99 us
  Pallas kernels: 0 us -> 157 us
  local copies, waits for them, and re-layouts: 163 us -> 6.95 us
  matrix products: 158 us -> 36.6 us
  other arithmetic: 109 us -> 3.61 us
    ppermute x64 -> x4, waiting for transfers between devices: 1120 us -> 0.01 us  [the longest x1 0.01 us: layer_block(): lax.ppermute(tail, ('sp', 'tp'), edge_same)]
    ppermute x64 -> x4, starting transfers between devices: 443 us -> 5.99 us  [the longest x1 3.25 us: layer_block(): lax.ppermute(tail, ('sp', 'tp'), edge_same)]
    pallas_call x0 -> x4, Pallas kernels: none -> 157 us  [the longest x1 69.8 us: layer_block(): pl.pallas_call(functools.partial(project_conv_kernel, dims), grid_spec=pl...]
    reduce_scatter x1 -> x0, waiting for transfers between devices: 154 us -> none  [layer_block(): lax.psum_scatter(partial_out, 'tp', scatter_dimension=0, tiled=True)]
    dot_general x8 -> x2, matrix products: 158 us -> 36.6 us  [the longest x1 19.5 us: layer_block(): jnp.dot(rows_own, w_out, preferred_element_type=F32)]
    reshape x4 -> x0, local copies, waits for them, and re-layouts: 51 us -> none  [the longest x2 50.8 us: layer_block(): (y_diag + y_off).reshape(seq_blk, n_groups, head_rep, head_dim)]
    convert_element_type x6 -> x1, other arithmetic: 49.7 us -> 0.92 us  [layer_block(): one_hot = (lane_head[:, None] == head_of[None, :]).astype(BF16)]
    unnamed x29 -> x12, local copies, waits for them, and re-layouts: 44.3 us -> 2.48 us
  transfers between devices with their start and end apart: 66 -> 4, of which waited for: 65 -> 0; matrix products, arithmetic and copies ran while one was open for 3% -> 4% of each run, Pallas kernels for 0% -> 5%
where the time goes in v2:
time: 211 us; the launch traced here: 210 us
  Pallas kernels  157 us (74%)
  matrix products  36.6 us (17%)
  local copies, waits for them, and re-layouts  6.95 us (3%)
  starting transfers between devices  5.99 us (3%)
  other arithmetic  3.61 us (2%)
    pallas_call x1, Pallas kernels, layer_block(): pl.pallas_call(functools.partial(project_conv_kernel, dims), grid_spec=pl...  69.8 us
    pallas_call x1, Pallas kernels, layer_block(): pl.pallas_call(functools.partial(gate_ssd_kernel, dims, sp_size), grid=(n...  66.5 us
    pallas_call x2, Pallas kernels, finish(): pl.pallas_call(functools.partial(gate_norm_kernel, dims), grid_spec=pltpu...  20.6 us
    dot_general x1, matrix products, layer_block(): jnp.dot(rows_own, w_out, preferred_element_type=F32)  19.5 us
    dot_general x1, matrix products, layer_block(): part_oth = jnp.dot(rows_oth, w_out, preferred_element_type=F32).astype(BF16)  17.1 us
  transfers between devices with their start and end apart: 4, of which 0 were waited for; matrix products, arithmetic and copies ran while one was open for 4% of the time, Pallas kernels for 5%

profile of v2, /device:TPU:1, one launch (start us, length us, event | category | flops | bytes accessed | tf_op | source)
XLA Modules:
  0.0 210.2 jit_solution(1051600042665654257)
XLA Ops:
  0.0 1.4 collective-permute-start
  1.4 0.9 slice.3
  2.3 3.3 %collective-permute-start.2 = (bf16[16,2688]{1,0:T(8,128)(2,1)S(1)}, bf16[16,2688]{1,0:T(8,128)(2,1)S(1)}, u32[]{:S(2)}, u32[]{:S(2)}) collective-permute-start(bf16[16,2688]{1,0:T(8,128)(2,1)S(1)} %slice.3), channel_id=1, source_target_pairs={{1,3},{3,5},{5,7},{7,9},{9,11},{11,13},{13,15},{15,17},{17,19},{19... | collective-permute-start | bytes 258056 | tf_op jit(solution)/shard_map/ppermute | solution.py:367
  5.5 1.3 collective-permute-start.1
  6.8 0.7 tile.4
  7.5 0.1 broadcast_in_dim_tile.6
  7.6 0.7 tile.5
  8.2 0.1 broadcast_in_dim_tile.7
  8.3 0.7 broadcast_in_dim.15.nw_ref
  9.0 0.7 convert_bitcast_fusion.1
  9.7 0.6 copy.11
  10.3 0.7 broadcast_in_dim.14
  11.0 0.7 broadcast_in_dim_reshape.3.ds_ref
  11.7 0.7 convert_bitcast_fusion
  12.5 0.6 copy.10
  13.1 0.9 compare_convert_fusion.oh_ref
  14.0 0.6 pad_maximum_fusion.hp_ref
  14.6 0.0 collective-permute-done.2
  14.6 0.0 collective-permute-done.1
  14.6 0.7 add.30.halo_ref
  15.3 0.0 collective-permute-done.oth_ref
  15.3 69.8 %project_conv_states.1 = (bf16[2048,3072]{1,0:T(8,128)(2,1)}, f32[3,2048,128]{2,1,0:T(8,128)}, f32[64,40,128]{2,1,0:T(8,128)}) custom-call(s32[1]{0:T(128)} %bitcast.tp_ref, bf16[1024,2688]{1,0:T(8,128)(2,1)} %own_ref.3, bf16[1024,2688]{1,0:T(8,128)(2,1)} %collective-permute-done.oth_ref, bf16[16,2688]{1,0:T(8,128)(2,1)} %add.30.halo_ref, ...), custom_call_target="tpu_custom_call" | custom-call | flops 33822867456 | bytes 16515072 | tf_op jit(solution)/shard_map/project_conv_states/pallas_call | solution.py:380
  85.1 0.0 copy-start
  85.1 66.5 %gate_ssd_exchange.1 = (bf16[2,1024,2048]{2,1,0:T(8,128)(2,1)}, f32[2048,2048]{1,0:T(8,128)}, f32[64,32,128]{2,1,0:T(8,128)}) custom-call(f32[64,40,128]{2,1,0:T(8,128)} %get-tuple-element.11.end_ref, bf16[1024,2688]{1,0:T(8,128)(2,1)} %own_ref.3, bf16[1024,2688]{1,0:T(8,128)(2,1)} %collective-permute-done.oth_ref, bf16[5152,2688]{1,0:T(8,128)(2,1)} %bitcast.14, ...), custom_call_target="tpu_custom_call" | custom-call | tf_op jit(solution)/shard_map/gate_ssd_exchange/pallas_call | solution.py:428
  151.7 1.2 copy-done.2
  152.9 10.3 %gate_norm.3 = bf16[1024,2048]{1,0:T(8,128)(2,1)} custom-call(s32[1]{0:T(128)} %bitcast.tp_ref, f32[2048,2048]{1,0:T(8,128)} %get-tuple-element.14.y_ref, bf16[2048,3072]{1,0:T(8,128)(2,1)} %get-tuple-element.12.act_ref.c0_ref.c1_ref.c2_ref.c3_ref, bf16[2048,3072]{1,0:T(8,128)(2,1)} %get-tuple-element.12.act_ref.c0_ref.c1_ref.c2_ref.c3_ref, ...), custom_call_target="tpu_custom_call" | custom-call | flops 5637144576 | bytes 20971520 | tf_op jit(solution)/shard_map/gate_norm/pallas_call | solution.py:472
  163.2 17.1 %convolution_convert_fusion = bf16[1024,2688]{1,0:T(8,128)(2,1)S(1)} fusion(bf16[1024,2048]{1,0:T(8,128)(2,1)} %gate_norm.3, bf16[2048,2688]{1,0:T(8,128)(2,1)} %param.17), kind=kOutput, calls=%fused_computation.1 | convolution fusion | flops 11277041664 | bytes 20709376 | tf_op jit(solution)/shard_map/dot_general | solution.py:494
  180.3 0.1 collective-permute-start.3
  180.4 10.2 %gate_norm.2 = bf16[1024,2048]{1,0:T(8,128)(2,1)} custom-call(s32[1]{0:T(128)} %bitcast.tp_ref, f32[2048,2048]{1,0:T(8,128)} %get-tuple-element.14.y_ref, bf16[2048,3072]{1,0:T(8,128)(2,1)} %get-tuple-element.12.act_ref.c0_ref.c1_ref.c2_ref.c3_ref, bf16[2048,3072]{1,0:T(8,128)(2,1)} %get-tuple-element.12.act_ref.c0_ref.c1_ref.c2_ref.c3_ref, ...), custom_call_target="tpu_custom_call" | custom-call | flops 5637144576 | bytes 20971520 | tf_op jit(solution)/shard_map/gate_norm/pallas_call | solution.py:472
  190.6 0.0 collective-permute-done.3
  190.6 0.0 slice-done.1
  190.7 19.5 %add_convert_fusion = bf16[1024,2688]{1,0:T(8,128)(2,1)} fusion(bf16[1024,2688]{1,0:T(8,128)(2,1)} %collective-permute-done.3, bf16[1024,2688]{1,0:T(8,128)(2,1)S(1)} %bitcast.16, bf16[1024,2048]{1,0:T(8,128)(2,1)} %gate_norm.2, bf16[2048,2688]{1,0:T(8,128)(2,1)} %param.17), kind=kOutput, calls=%fused_computation | convolution fusion | flops 11290804224 | bytes 31719424 | tf_op jit(solution)/shard_map/dot_general | solution.py:497
  (10 shorter events, 0.0 us)
Async XLA Ops:
  0.0 15.3 %collective-permute-start = (bf16[1024,2688]{1,0:T(8,128)(2,1)}, bf16[1024,2688]{1,0:T(8,128)(2,1)}, u32[]{:S(2)}, u32[]{:S(2)}) collective-permute-start(bf16[1024,2688]{1,0:T(8,128)(2,1)} %own_ref.3), channel_id=1, source_target_pairs={{0,1},{1,0},{2,3},{3,2},{4,5},{5,4},{6,7},{7,6},{8,9},{9,8},{10,11... | collective-permute-start | bytes 16515080 | tf_op jit(solution)/shard_map/ppermute | solution.py:363
  2.3 12.3 %collective-permute-start.2 = (bf16[16,2688]{1,0:T(8,128)(2,1)S(1)}, bf16[16,2688]{1,0:T(8,128)(2,1)S(1)}, u32[]{:S(2)}, u32[]{:S(2)}) collective-permute-start(bf16[16,2688]{1,0:T(8,128)(2,1)S(1)} %slice.3), channel_id=1, source_target_pairs={{1,3},{3,5},{5,7},{7,9},{9,11},{11,13},{13,15},{15,17},{17,19},{19... | collective-permute-start | bytes 258056 | tf_op jit(solution)/shard_map/ppermute | solution.py:367
  5.5 9.1 %collective-permute-start.1 = (bf16[16,2688]{1,0:T(8,128)(2,1)S(1)}, bf16[16,2688]{1,0:T(8,128)(2,1)S(1)}, u32[]{:S(2)}, u32[]{:S(2)}) collective-permute-start(bf16[16,2688]{1,0:T(8,128)(2,1)S(1)} %slice.3), channel_id=1, source_target_pairs={{1,2},{3,4},{5,6},{7,8},{9,10},{11,12},{13,14},{15,16},{17,18},{19... | collective-permute-start | bytes 258056 | tf_op jit(solution)/shard_map/ppermute | solution.py:367
  85.1 66.5 %copy-start = (f32[3,2048,128]{2,1,0:T(8,128)S(1)}, f32[3,2048,128]{2,1,0:T(8,128)}, u32[]{:S(2)}) copy-start(f32[3,2048,128]{2,1,0:T(8,128)} %get-tuple-element.13.dts_ref) | copy-start | bytes 9437188
  85.1 66.5 %copy-start.1 = (bf16[128,2048]{1,0:T(8,128)(2,1)S(1)}, bf16[128,2048]{1,0:T(8,128)(2,1)}, u32[]{:S(2)}) copy-start(bf16[128,2048]{1,0:T(8,128)(2,1)} %compare_convert_fusion.oh_ref) | copy-start | bytes 1572868
  151.6 1.2 copy-start.2
  152.9 37.8 %slice-start = ((s8[5505024]{0:T(1024)(128)(4,1)}), s8[4194304]{0:T(1024)(128)(4,1)S(1)}, s32[]{:S(2)}) async-start(s8[5505024]{0:T(1024)(128)(4,1)} %bitcast.15), calls=%async_computation | async-start | bytes 8388608
  163.2 27.4 %slice-start.1 = ((s8[5505024]{0:T(1024)(128)(4,1)}), s8[1310720]{0:T(1024)(128)(4,1)S(1)}, s32[]{:S(2)}) async-start(s8[5505024]{0:T(1024)(128)(4,1)} %bitcast.15), calls=%async_computation.1 | async-start | bytes 2621440
  180.3 10.3 %collective-permute-start.3 = (bf16[1024,2688]{1,0:T(8,128)(2,1)S(1)}, bf16[1024,2688]{1,0:T(8,128)(2,1)}, u32[]{:S(2)}, u32[]{:S(2)}) collective-permute-start(bf16[1024,2688]{1,0:T(8,128)(2,1)S(1)} %convolution_convert_fusion), channel_id=1, source_target_pairs={{0,1},{1,0},{2,3},{3,2},{4,5},{5,4},{6,7},{7,6},{8,9},{9,8},{10,11... | collective-permute-start | bytes 16515080 | tf_op jit(solution)/shard_map/ppermute | solution.py:495

commit v3 on v2

--- a/solution.py
+++ b/solution.py
@@ -10,6 +10,7 @@
 SEG = 128
 SUB = 256
 HALO = 16
+EXCHANGE = True
 NORM_EPS = 1e-5
 LANES = 128
 PIECE_PAD = 8
@@ -314,27 +315,81 @@
         in_ref[...] = received[...]
 
 
-def gate_norm_kernel(dims, tp_ref, y_ref, c0_ref, c1_ref, c2_ref, c3_ref, z_ref, dts_ref, in_ref, oh_ref, nw_ref, o_ref, state):
+def gate_out_kernel(dims, y_ref, c0_ref, c1_ref, c2_ref, c3_ref, z_ref, dts_ref, in_ref, oh_ref, nw_ref, wo_hbm, tok_ref, out_ref,
+                    wo_ref, state, o_next, o_prev, parts, received, wsem, send_sems, recv_sems):
     n_groups, group_inner, n_state, head_rep, half = dims
-
-    @pl.when(pl.program_id(0) == 0)
-    def _():
-        n_tiles = n_groups * group_inner // LANES
-        quarters = in_ref.shape[0] // n_tiles
+    step_id = pl.program_id(0)
+    n_tiles = half // SUB
+    peer = {"tp": 1 - lax.axis_index("tp")} if EXCHANGE else None
+
+    def send(k):
+        return pltpu.make_async_remote_copy(
+            src_ref=parts.at[k], dst_ref=received.at[k], send_sem=send_sems.at[k], recv_sem=recv_sems.at[k],
+            device_id=peer, device_id_type=pl.DeviceIdType.MESH)
+
+    def gate_rows():
+        from_start = spread(jnp.exp2(dts_ref[0]), oh_ref[...])
+        for g, c_ref in enumerate((c0_ref, c1_ref, c2_ref, c3_ref)):
+            i0, i1 = g * group_inner, (g + 1) * group_inner
+            y_in = jnp.dot(c_ref[...], state[:, i0:i1], preferred_element_type=F32)
+            y_ssd = y_ref[:, i0:i1] + y_in * from_start[:, i0:i1]
+            gate = z_ref[0, :, i0:i1].astype(F32)
+            gated = y_ssd * (gate / (1.0 + jnp.exp(-gate)))
+            inv_rms = lax.rsqrt(jnp.mean(gated * gated, axis=-1, keepdims=True) + NORM_EPS)
+            o_next[:, i0:i1] = (gated * inv_rms * nw_ref[0:1, i0:i1].astype(F32)).astype(BF16)
+
+    def out_rows():
+        parts[jnp.minimum(step_id - 1, n_tiles)] = jnp.dot(o_prev[...], wo_ref[...], preferred_element_type=F32).astype(BF16)
+
+    wo_copy = pltpu.make_async_copy(wo_hbm, wo_ref, wsem)
+
+    @pl.when(step_id == 0)
+    def _():
+        wo_copy.start()
+        if EXCHANGE:
+            pl.semaphore_signal(pltpu.get_barrier_semaphore(), inc=1, device_id=peer, device_id_type=pl.DeviceIdType.MESH)
+        lane_tiles = n_groups * group_inner // LANES
+        quarters = in_ref.shape[0] // lane_tiles
         depth = n_state // quarters
-        for t in range(n_tiles):
+        for t in range(lane_tiles):
             for q in range(quarters):
                 state[q * depth:(q + 1) * depth, t * LANES:(t + 1) * LANES] = in_ref[t * quarters + q].astype(BF16)
-
-    from_start = spread(jnp.exp2(dts_ref[0]), oh_ref[...])
-    for g, c_ref in enumerate((c0_ref, c1_ref, c2_ref, c3_ref)):
-        i0, i1 = g * group_inner, (g + 1) * group_inner
-        y_in = jnp.dot(c_ref[...], state[:, i0:i1], preferred_element_type=F32)
-        y_ssd = y_ref[:, i0:i1] + y_in * from_start[:, i0:i1]
-        gate = z_ref[0, :, i0:i1].astype(F32)
-        gated = y_ssd * (gate / (1.0 + jnp.exp(-gate)))
-        inv_rms = lax.rsqrt(jnp.mean(gated * gated, axis=-1, keepdims=True) + NORM_EPS)
-        o_ref[:, i0:i1] = (gated * inv_rms * nw_ref[0:1, i0:i1].astype(F32)).astype(BF16)
+        gate_rows()
+        wo_copy.wait()
+        if EXCHANGE:
+            pl.semaphore_wait(pltpu.get_barrier_semaphore(), 1)
+
+    @pl.when((step_id > 0) & (step_id < 2 * n_tiles))
+    def _():
+        out_rows()
+        gate_rows()
+
+    @pl.when(step_id == 2 * n_tiles)
+    def _():
+        out_rows()
+
+    o_prev[...] = o_next[...]
+
+    if EXCHANGE:
+        for k in range(n_tiles):
+            @pl.when(step_id == k + 1)
+            def _(k=k):
+                send(k).start()
+
+            @pl.when(step_id == n_tiles + 1 + k)
+            def _(k=k):
+                send(k).wait_recv()
+
+    @pl.when(step_id > n_tiles)
+    def _():
+        got = received[jnp.maximum(step_id - n_tiles - 1, 0)]
+        out_ref[...] = (tok_ref[...].astype(F32) + parts[n_tiles].astype(F32) + got.astype(F32)).astype(BF16)
+
+    if EXCHANGE:
+        @pl.when(step_id == 2 * n_tiles)
+        def _():
+            for k in range(n_tiles):
+                send(k).wait_send()
 
 
 def solution(mesh):
@@ -462,40 +517,53 @@
             name="gate_ssd_exchange",
         )(end_state, tokens, other, w_in_t, act, dts, one_hot, skip_row)
 
-        def finish(slot):
-            def at(i, tp):
-                return ((tp[0] + slot) % 2) * (half // SUB) + i
-
-            def c_spec(g):
-                return pl.BlockSpec((SUB, LANES), lambda i, tp: (at(i, tp), 6 * g + 5))
-
-            return pl.pallas_call(
-                functools.partial(gate_norm_kernel, dims),
-                grid_spec=pltpu.PrefetchScalarGridSpec(
-                    num_scalar_prefetch=1, grid=(half // SUB,),
-                    in_specs=[
-                        pl.BlockSpec((SUB, inner_dim), lambda i, tp: (at(i, tp), 0)),
-                        c_spec(0), c_spec(1), c_spec(2), c_spec(3),
-                        pl.BlockSpec((1, SUB, inner_dim), lambda i, tp: (slot, i, 0)),
-                        pl.BlockSpec((1, SUB, LANES), lambda i, tp: (2, at(i, tp), 0)),
-                        pl.BlockSpec((n_pieces, depth, LANES), lambda i, tp: (0, 0, 0)),
-                        pl.BlockSpec((LANES, inner_dim), lambda i, tp: (0, 0)),
-                        pl.BlockSpec((1, inner_dim), lambda i, tp: (0, 0)),
-                    ],
-                    out_specs=pl.BlockSpec((SUB, inner_dim), lambda i, tp: (i, 0)),
-                    scratch_shapes=[pltpu.VMEM((n_state, inner_dim), BF16)]),
-                out_shape=jax.ShapeDtypeStruct((half, inner_dim), BF16),
-                compiler_params=pltpu.CompilerParams(vmem_limit_bytes=48 * 2**20),
-                cost_estimate=pl.CostEstimate(flops=half * width * inner_dim, bytes_accessed=10 * half * inner_dim, transcendentals=0),
-                name="gate_norm",
-            )(tp_arr, y_local, act, act, act, act, gate_z, dts, incoming, one_hot, norm_w[None])
-
-        rows_oth = finish(1)
-        part_oth = jnp.dot(rows_oth, w_out, preferred_element_type=F32).astype(BF16)
-        received = lax.ppermute(part_oth, "tp", swap)
-        rows_own = finish(0)
-        part_own = lax.reduce_precision(jnp.dot(rows_own, w_out, preferred_element_type=F32), 8, 7)
-        return (tokens.astype(F32) + part_own + received.astype(F32)).astype(BF16)
+        n_tiles = half // SUB
+
+        def tile(i):
+            return jnp.minimum(i, 2 * n_tiles - 1)
+
+        def slot_of(i):
+            return 1 - tile(i) // n_tiles
+
+        def row_at(i):
+            return lax.rem(lax.axis_index("tp") + slot_of(i), 2) * n_tiles + lax.rem(tile(i), n_tiles)
+
+        def own_at(i):
+            return jnp.maximum(i - n_tiles - 1, 0)
+
+        def c_spec(g):
+            return pl.BlockSpec((SUB, LANES), lambda i: (row_at(i), 6 * g + 5))
+
+        return pl.pallas_call(
+            functools.partial(gate_out_kernel, dims),
+            grid=(2 * n_tiles + 1,),
+            in_specs=[
+                pl.BlockSpec((SUB, inner_dim), lambda i: (row_at(i), 0)),
+                c_spec(0), c_spec(1), c_spec(2), c_spec(3),
+                pl.BlockSpec((1, SUB, inner_dim), lambda i: (slot_of(i), lax.rem(tile(i), n_tiles), 0)),
+                pl.BlockSpec((1, SUB, LANES), lambda i: (2, row_at(i), 0)),
+                pl.BlockSpec((n_pieces, depth, LANES), lambda i: (0, 0, 0), **once),
+                pl.BlockSpec((LANES, inner_dim), lambda i: (0, 0), **once),
+                pl.BlockSpec((1, inner_dim), lambda i: (0, 0)),
+                any_spec,
+                pl.BlockSpec((SUB, width), lambda i: (own_at(i), 0)),
+            ],
+            out_specs=pl.BlockSpec((SUB, width), lambda i: (own_at(i), 0)),
+            out_shape=jax.ShapeDtypeStruct((half, width), BF16),
+            scratch_shapes=[
+                pltpu.VMEM((inner_dim, width), BF16),
+                pltpu.VMEM((n_state, inner_dim), BF16),
+                pltpu.VMEM((SUB, inner_dim), BF16),
+                pltpu.VMEM((SUB, inner_dim), BF16),
+                pltpu.VMEM((n_tiles + 1, SUB, width), BF16),
+                pltpu.VMEM((n_tiles, SUB, width), BF16),
+                pltpu.SemaphoreType.DMA,
+                pltpu.SemaphoreType.DMA((n_tiles,)),
+                pltpu.SemaphoreType.DMA((n_tiles,)),
+            ],
+            compiler_params=pltpu.CompilerParams(vmem_limit_bytes=limit, **(dict(collective_id=1, has_side_effects=True) if EXCHANGE else {})),
+            name="gate_out_swap",
+        )(y_local, act, act, act, act, gate_z, dts, incoming, one_hot, norm_w[None], w_out, tokens)
 
     return jax.shard_map(
         layer_block,

time: 211 us -> 206 us (0.976)
  matrix products: 36.6 us -> 0 us
  Pallas kernels: 157 us -> 183 us
  local copies, waits for them, and re-layouts: 6.95 us -> 11.7 us
    dot_general x2 -> x0, matrix products: 36.6 us -> none  [the longest x1 19.5 us: layer_block(): jnp.dot(rows_own, w_out, preferred_element_type=F32)]
    pallas_call x2 -> x1, Pallas kernels: 20.6 us -> 48 us  [layer_block(): pl.pallas_call(functools.partial(gate_out_kernel, dims), grid=(2 * n_tile...]
    unnamed x12 -> x3, local copies, waits for them, and re-layouts: 2.48 us -> 6.63 us
  transfers between devices with their start and end apart: 4 -> 3, of which waited for: 0 -> 0; matrix products, arithmetic and copies ran while one was open for 4% -> 5% of each run, Pallas kernels for 5% -> 0%
where the time goes in v3:
time: 206 us
  Pallas kernels  183 us (89%)
  local copies, waits for them, and re-layouts  11.7 us (6%)
  starting transfers between devices  7.62 us (4%)
  other arithmetic  3.6 us (2%)
    pallas_call x1, Pallas kernels, layer_block(): pl.pallas_call(functools.partial(project_conv_kernel, dims), grid_spec=pl...  68.6 us
    pallas_call x1, Pallas kernels, layer_block(): pl.pallas_call(functools.partial(gate_ssd_kernel, dims, sp_size), grid=(n...  66.1 us
    pallas_call x1, Pallas kernels, layer_block(): pl.pallas_call(functools.partial(gate_out_kernel, dims), grid=(2 * n_tile...  48 us
    unnamed x3, local copies, waits for them, and re-layouts  6.63 us
  transfers between devices with their start and end apart: 3, of which 0 were waited for; matrix products, arithmetic and copies ran while one was open for 5% of the time, Pallas kernels for 0%

profile of v3, /device:TPU:1, one launch (start us, length us, event | category | flops | bytes accessed | tf_op | source)
XLA Modules:
  0.0 205.6 jit_solution(12779014054183748102)
XLA Ops:
  0.0 1.4 collective-permute-start
  1.4 0.9 slice.3
  2.3 3.1 %collective-permute-start.1 = (bf16[16,2688]{1,0:T(8,128)(2,1)S(1)}, bf16[16,2688]{1,0:T(8,128)(2,1)S(1)}, u32[]{:S(2)}, u32[]{:S(2)}) collective-permute-start(bf16[16,2688]{1,0:T(8,128)(2,1)S(1)} %slice.3), channel_id=1, source_target_pairs={{1,2},{3,4},{5,6},{7,8},{9,10},{11,12},{13,14},{15,16},{17,18},{19... | collective-permute-start | bytes 258056 | tf_op jit(solution)/shard_map/ppermute | solution.py:422
  5.4 3.1 %collective-permute-start.2 = (bf16[16,2688]{1,0:T(8,128)(2,1)S(1)}, bf16[16,2688]{1,0:T(8,128)(2,1)S(1)}, u32[]{:S(2)}, u32[]{:S(2)}) collective-permute-start(bf16[16,2688]{1,0:T(8,128)(2,1)S(1)} %slice.3), channel_id=1, source_target_pairs={{1,3},{3,5},{5,7},{7,9},{9,11},{11,13},{13,15},{15,17},{17,19},{19... | collective-permute-start | bytes 258056 | tf_op jit(solution)/shard_map/ppermute | solution.py:422
  8.5 0.7 convert_bitcast_fusion
  9.3 0.6 copy.10
  9.9 0.7 convert_bitcast_fusion.1
  10.6 0.6 copy.11
  11.2 0.7 tile.4
  11.9 0.1 broadcast_in_dim_tile.6
  12.0 0.7 tile.5
  12.6 0.1 broadcast_in_dim_tile.7
  12.7 0.7 broadcast_in_dim.13
  13.4 0.7 broadcast_in_dim_reshape.3.ds_ref
  14.1 1.3 broadcast_in_dim.14.nw_ref
  15.4 0.9 compare_convert_fusion.oh_ref
  16.3 0.6 pad_maximum_fusion.hp_ref
  16.9 0.0 collective-permute-done.1
  16.9 0.0 collective-permute-done.2
  16.9 0.6 add.22.halo_ref
  17.6 0.0 collective-permute-done.oth_ref
  17.6 68.6 %project_conv_states.1 = (bf16[2048,3072]{1,0:T(8,128)(2,1)}, f32[3,2048,128]{2,1,0:T(8,128)}, f32[64,40,128]{2,1,0:T(8,128)}) custom-call(s32[1]{0:T(128)} %bitcast.tp_ref, bf16[1024,2688]{1,0:T(8,128)(2,1)} %tok_ref.1, bf16[1024,2688]{1,0:T(8,128)(2,1)} %collective-permute-done.oth_ref, bf16[16,2688]{1,0:T(8,128)(2,1)} %add.22.halo_ref, ...), custom_call_target="tpu_custom_call" | custom-call | flops 33822867456 | bytes 16515072 | tf_op jit(solution)/shard_map/project_conv_states/pallas_call | solution.py:435
  86.2 66.1 %gate_ssd_exchange.1 = (bf16[2,1024,2048]{2,1,0:T(8,128)(2,1)}, f32[2048,2048]{1,0:T(8,128)}, f32[64,32,128]{2,1,0:T(8,128)}) custom-call(f32[64,40,128]{2,1,0:T(8,128)} %get-tuple-element.11.end_ref, bf16[1024,2688]{1,0:T(8,128)(2,1)} %tok_ref.1, bf16[1024,2688]{1,0:T(8,128)(2,1)} %collective-permute-done.oth_ref, bf16[5152,2688]{1,0:T(8,128)(2,1)} %bitcast.10, ...), custom_call_target="tpu_custom_call" | custom-call | tf_op jit(solution)/shard_map/gate_ssd_exchange/pallas_call | solution.py:483
  152.2 48.0 %gate_out_swap.1 = bf16[1024,2688]{1,0:T(8,128)(2,1)} custom-call(f32[2048,2048]{1,0:T(8,128)} %get-tuple-element.14.y_ref, bf16[2048,3072]{1,0:T(8,128)(2,1)} %get-tuple-element.12.act_ref.c0_ref.c1_ref.c2_ref.c3_ref, bf16[2048,3072]{1,0:T(8,128)(2,1)} %get-tuple-element.12.act_ref.c0_ref.c1_ref.c2_ref.c3_ref, ...), custom_call_target="tpu_custom_call" | custom-call | tf_op jit(solution)/shard_map/gate_out_swap/pallas_call | solution.py:537
  200.2 5.4 %copy.13 = bf16[1024,2688]{1,0:T(8,128)(2,1)} copy(bf16[1024,2688]{1,0:T(8,128)(2,1)} %gate_out_swap.1) | data formatting | bytes 11010048
  (2 shorter events, 0.0 us)
Async XLA Ops:
  0.0 17.6 %collective-permute-start = (bf16[1024,2688]{1,0:T(8,128)(2,1)}, bf16[1024,2688]{1,0:T(8,128)(2,1)}, u32[]{:S(2)}, u32[]{:S(2)}) collective-permute-start(bf16[1024,2688]{1,0:T(8,128)(2,1)} %tok_ref.1), channel_id=1, source_target_pairs={{0,1},{1,0},{2,3},{3,2},{4,5},{5,4},{6,7},{7,6},{8,9},{9,8},{10,11... | collective-permute-start | bytes 16515080 | tf_op jit(solution)/shard_map/ppermute | solution.py:418
  2.3 14.7 %collective-permute-start.1 = (bf16[16,2688]{1,0:T(8,128)(2,1)S(1)}, bf16[16,2688]{1,0:T(8,128)(2,1)S(1)}, u32[]{:S(2)}, u32[]{:S(2)}) collective-permute-start(bf16[16,2688]{1,0:T(8,128)(2,1)S(1)} %slice.3), channel_id=1, source_target_pairs={{1,2},{3,4},{5,6},{7,8},{9,10},{11,12},{13,14},{15,16},{17,18},{19... | collective-permute-start | bytes 258056 | tf_op jit(solution)/shard_map/ppermute | solution.py:422
  5.4 11.5 %collective-permute-start.2 = (bf16[16,2688]{1,0:T(8,128)(2,1)S(1)}, bf16[16,2688]{1,0:T(8,128)(2,1)S(1)}, u32[]{:S(2)}, u32[]{:S(2)}) collective-permute-start(bf16[16,2688]{1,0:T(8,128)(2,1)S(1)} %slice.3), channel_id=1, source_target_pairs={{1,3},{3,5},{5,7},{7,9},{9,11},{11,13},{13,15},{15,17},{17,19},{19... | collective-permute-start | bytes 258056 | tf_op jit(solution)/shard_map/ppermute | solution.py:422

commit v4 on v3

--- a/solution.py
+++ b/solution.py
@@ -45,7 +45,7 @@
                         cw_ref, cb_ref, hp_ref, oh_ref, act_ref, dts_ref, end_ref,
                         x_buf, weights, w_dt, ext0, ext1, ext2, ext3, state, total, sems, wsems, dsems):
     n_groups, group_inner, n_state, head_rep, half = dims
-    group_id, half_id = pl.program_id(0), pl.program_id(1)
+    group_id = pl.program_id(0)
     n_heads = n_groups * head_rep
     exts = (ext0, ext1, ext2, ext3)
 
@@ -57,7 +57,7 @@
             lambda: pltpu.make_async_copy(second, x_buf.at[1, pl.ds(HALO, half)], sems.at[3]),
         ]
 
-    start = (group_id == 0) & (half_id == 0)
+    start = group_id == 0
 
     @pl.when(start & (tp_ref[0] == 0))
     def _():
@@ -86,26 +86,16 @@
         for c in copies(own_ref, oth_ref)[:2]:
             c().wait()
 
-    @pl.when((group_id == 0) & (half_id == 1))
-    def _():
-        for c in copies(own_ref, oth_ref)[2:]:
-            c().wait()
-
-    @pl.when(half_id == 0)
-    def _():
-        weight_copy(wt_ref, weights, wsems, group_id, group_cols, group_inner).wait()
-        state[...] = jnp.zeros_like(state)
-
-    @pl.when((half_id == 0) & (group_id < n_groups - 1))
+    weight_copy(wt_ref, weights, wsems, group_id, group_cols, group_inner).wait()
+    state[...] = jnp.zeros_like(state)
+
+    @pl.when(group_id < n_groups - 1)
     def _():
         weight_copy(wt_ref, weights, wsems, group_id + 1, group_cols, group_inner).start()
 
     w_slot = lax.rem(group_id, 2)
 
-    row0 = half_id * half
-
-    @pl.when(group_id == 0)
-    def _():
+    def steps_of(half_id):
         def step(s, carry):
             at = pl.ds(pl.multiple_of(HALO + s * SUB, 16), SUB)
             raw = lax.dot_general(x_buf[half_id, at, :], w_dt[...], CONTRACT_LAST, preferred_element_type=F32).astype(BF16).astype(F32)
@@ -118,7 +108,7 @@
             for q in range(SUB // SEG):
                 lo, hi = q * SEG, (q + 1) * SEG
                 cum = jnp.dot(tri, log_decay[lo:hi], precision=lax.Precision.HIGHEST, preferred_element_type=F32)
-                out = pl.ds(pl.multiple_of(row0 + s * SUB + lo, SEG), SEG)
+                out = pl.ds(pl.multiple_of(half_id * half + s * SUB + lo, SEG), SEG)
                 dts_ref[0, out, :] = dt_step[lo:hi]
                 dts_ref[1, out, :] = cum
                 dts_ref[2, out, :] = cum + total[...]
@@ -126,16 +116,20 @@
             return carry
         lax.fori_loop(0, half // SUB, step, 0)
 
+    @pl.when(group_id == 0)
+    def _():
+        steps_of(0)
+
     n_cols = weights.shape[1] // LANES
 
-    def matmul(s):
+    def matmul(half_id, s):
         lo = 0 if s == 0 else HALO
         rows = x_buf[half_id, s * SUB + lo:HALO + (s + 1) * SUB, :]
         raw = lax.dot_general(rows, weights[w_slot], CONTRACT_LAST, preferred_element_type=F32).astype(BF16).astype(F32)
         for t in range(n_cols):
             exts[s][t, lo:HALO + SUB] = raw[:, t * LANES:(t + 1) * LANES]
 
-    def convolved(s, t):
+    def convolved(half_id, s, t):
         ext = exts[s]
         if s > 0:
             ext[t, 8:HALO] = exts[s - 1][t, HALO + SUB - 8:HALO + SUB]
@@ -144,43 +138,48 @@
         for k in range(1, 4):
             acc = acc + ext[t, HALO - 3 + k:HALO - 3 + k + SUB] * cw_ref[k:k + 1, lanes]
         act = (acc / (1.0 + jnp.exp(-acc))).astype(BF16)
-        act_ref[s * SUB:(s + 1) * SUB, lanes] = act
+        act_ref[half_id * half + s * SUB:half_id * half + (s + 1) * SUB, lanes] = act
         return act
 
-    def vector(s):
+    def vector(half_id, s):
         n_x = group_inner // LANES
-        b_all = convolved(s, n_x)
-        convolved(s, n_x + 1)
-        at = pl.ds(pl.multiple_of(row0 + s * SUB, SUB), SUB)
+        b_all = convolved(half_id, s, n_x)
+        convolved(half_id, s, n_x + 1)
+        at = slice(half_id * half + s * SUB, half_id * half + (s + 1) * SUB)
         dt_step, cum = dts_ref[0, at, :], dts_ref[1, at, :]
         ends = [cum[(q + 1) * SEG - 1:(q + 1) * SEG] for q in range(SUB // SEG)]
         last = jnp.concatenate([jnp.broadcast_to(e, (SEG, LANES)) for e in ends], axis=0)
         end_w = spread(jnp.exp2(last - cum) * dt_step, oh_ref[...])
         decay = spread(jnp.exp2(jnp.concatenate([jnp.broadcast_to(e, (8, LANES)) for e in ends], axis=0)), oh_ref[...])
-        weighted = [(convolved(s, t).astype(F32) * end_w[:, t * LANES:(t + 1) * LANES]).astype(BF16) for t in range(n_x)]
+        weighted = [(convolved(half_id, s, t).astype(F32) * end_w[:, t * LANES:(t + 1) * LANES]).astype(BF16) for t in range(n_x)]
         weighted = jnp.concatenate(weighted, axis=1)
         for q in range(SUB // SEG):
             lo, hi = q * SEG, (q + 1) * SEG
             new = lax.dot_general(b_all[lo:hi], weighted[lo:hi], (((0,), (0,)), ((), ())), preferred_element_type=F32)
             state[...] = state[...] * decay[8 * q:8 * q + 1] + new
 
-    matmul(0)
-    for s in range(1, half // SUB):
-        matmul(s)
-        vector(s - 1)
-    vector(half // SUB - 1)
-
-    @pl.when(half_id == 1)
-    def _():
-        decay = spread(jnp.exp2(jnp.broadcast_to(total[...], (8, LANES))), oh_ref[...])
-        n_tiles = group_inner // LANES
-        quarters = end_ref.shape[0] // (n_groups * n_tiles)
-        depth = n_state // quarters
-        for t in range(n_tiles):
-            for q in range(quarters):
-                piece = (group_id * n_tiles + t) * quarters + q
-                end_ref[piece, 0:depth] = state[q * depth:(q + 1) * depth, t * LANES:(t + 1) * LANES]
-                end_ref[piece, depth:depth + PIECE_PAD] = decay[:, t * LANES:(t + 1) * LANES]
+    order = [(h, s) for h in range(2) for s in range(half // SUB)]
+    matmul(*order[0])
+    for k in range(1, len(order)):
+        if order[k] == (1, 0):
+            @pl.when(group_id == 0)
+            def _():
+                for c in copies(own_ref, oth_ref)[2:]:
+                    c().wait()
+                steps_of(1)
+        matmul(*order[k])
+        vector(*order[k - 1])
+    vector(*order[-1])
+
+    decay = spread(jnp.exp2(jnp.broadcast_to(total[...], (8, LANES))), oh_ref[...])
+    n_tiles = group_inner // LANES
+    quarters = end_ref.shape[0] // (n_groups * n_tiles)
+    depth = n_state // quarters
+    for t in range(n_tiles):
+        for q in range(quarters):
+            piece = (group_id * n_tiles + t) * quarters + q
+            end_ref[piece, 0:depth] = state[q * depth:(q + 1) * depth, t * LANES:(t + 1) * LANES]
+            end_ref[piece, depth:depth + PIECE_PAD] = decay[:, t * LANES:(t + 1) * LANES]
 
 
 def gate_ssd_kernel(dims, sp_size, end_ref, own_ref, oth_ref, wt_ref, act_ref, dts_ref, oh_ref, ds_ref, z_ref, y_ref, in_ref,
@@ -194,6 +193,7 @@
     n_z = 2 * n_groups
     me = lax.axis_index("sp")
     others = pl.ds(0, sp_size - 1)
+    sent = pl.ds(0, depth + 1)
     mesh_id = pl.DeviceIdType.MESH
 
     def x_copy(k):
@@ -219,7 +219,7 @@
         def send_out(k, carry):
             peer = lax.rem(me + k, sp_size)
             pltpu.make_async_remote_copy(
-                src_ref=end_ref.at[peer], dst_ref=gathered.at[me], send_sem=send_sem, recv_sem=recv_sem,
+                src_ref=end_ref.at[peer, sent], dst_ref=gathered.at[me, sent], send_sem=send_sem, recv_sem=recv_sem,
                 device_id={"sp": peer}, device_id_type=mesh_id).start()
             return carry
 
@@ -227,15 +227,19 @@
 
     @pl.when(step_id == n_z)
     def _():
-        pltpu.make_async_copy(end_ref.at[others], gathered.at[others], recv_sem).wait()
-        pltpu.make_async_copy(end_ref.at[others], gathered.at[others], send_sem).wait()
+        state[...] = jnp.zeros_like(state)
+
+    @pl.when(step_id == n_z + 2)
+    def _():
+        pltpu.make_async_copy(end_ref.at[others, sent], gathered.at[others, sent], recv_sem).wait()
+        pltpu.make_async_copy(end_ref.at[others, sent], gathered.at[others, sent], send_sem).wait()
         gathered[me] = end_ref[me]
 
         def scan_step(j, carry):
             starts[j] = carry
             return gathered[j, depth:depth + 1] * carry + gathered[j, 0:depth]
 
-        lax.fori_loop(0, sp_size, scan_step, jnp.zeros((depth, LANES), F32))
+        lax.fori_loop(0, sp_size, scan_step, jnp.zeros((depth, LANES), F32), unroll=4)
 
         def send_back(k, carry):
             peer = lax.rem(me + k, sp_size)
@@ -245,7 +249,6 @@
             return carry
 
         lax.fori_loop(1, sp_size, send_back, 0)
-        state[...] = jnp.zeros_like(state)
 
     @pl.when(step_id < n_z)
     def _():
@@ -271,9 +274,8 @@
         dt_step = dts_ref[0]
         cum = dts_ref[1]
         seg_total = cum[SEG - 1:SEG]
-        end_w = spread(jnp.exp2(seg_total - cum) * dt_step, oh_ref[...])
-        from_start = spread(jnp.exp2(cum), oh_ref[...])
-        seg_decay = from_start[SEG - 1:SEG]
+        end_v = jnp.exp2(seg_total - cum) * dt_step
+        start_v = jnp.exp2(cum)
         lane = lax.broadcasted_iota(jnp.int32, (SEG, LANES), 1)
         flipped = jnp.where(lane < n_heads, cum, dt_step).T
         row_id = lax.broadcasted_iota(jnp.int32, (SEG, SEG), 0)
@@ -284,10 +286,14 @@
             c0 = g * conv_cols
             i0, i1 = g * group_inner, (g + 1) * group_inner
             x_mat = act_ref[:, c0:c0 + group_inner]
+            end_w = spread(end_v, oh_ref[:, i0:i1])
+            from_start = spread(start_v, oh_ref[:, i0:i1])
             b_mat = act_ref[:, c0 + group_inner:c0 + group_inner + n_state]
             c_mat = act_ref[:, c0 + group_inner + n_state:c0 + conv_cols]
             c_dot_b = lax.dot_general(c_mat, b_mat, (((1,), (1,)), ((), ())), preferred_element_type=F32)
-            diag = []
+            held = state[:, i0:i1]
+            x_wide = x_mat.astype(F32)
+            y_rest = jnp.dot(c_mat, held.astype(BF16), preferred_element_type=F32) * from_start + ds_ref[0:1, i0:i1] * x_wide
             for pair in range(head_rep // 2):
                 scores = []
                 for h in (g * head_rep + 2 * pair, g * head_rep + 2 * pair + 1):
@@ -297,15 +303,11 @@
                 x_pair = x_mat[:, pair * LANES:(pair + 1) * LANES]
                 zero = jnp.zeros_like(x_pair)
                 x_both = jnp.concatenate([jnp.where(first_half, x_pair, zero), jnp.where(first_half, zero, x_pair)], axis=0)
-                diag.append(jnp.dot(jnp.concatenate(scores, axis=1), x_both, preferred_element_type=F32))
-            y_diag = jnp.concatenate(diag, axis=1)
-            held = state[:, i0:i1]
-            y_off = jnp.dot(c_mat, held.astype(BF16), preferred_element_type=F32) * from_start[:, i0:i1]
-            x_wide = x_mat.astype(F32)
-            y_ref[:, i0:i1] = y_diag + y_off + ds_ref[0:1, i0:i1] * x_wide
-            weighted = (x_wide * end_w[:, i0:i1]).astype(BF16)
+                y_diag = jnp.dot(jnp.concatenate(scores, axis=1), x_both, preferred_element_type=F32)
+                y_ref[:, i0 + pair * LANES:i0 + (pair + 1) * LANES] = y_rest[:, pair * LANES:(pair + 1) * LANES] + y_diag
+            weighted = (x_wide * end_w).astype(BF16)
             new = lax.dot_general(b_mat, weighted, (((0,), (0,)), ((), ())), preferred_element_type=F32)
-            state[:, i0:i1] = held * seg_decay[:, i0:i1] + new
+            state[:, i0:i1] = held * from_start[SEG - 1:SEG] + new
 
     @pl.when(step_id == pl.num_programs(0) - 1)
     def _():
@@ -435,18 +437,18 @@
         act, dts, end_state = pl.pallas_call(
             functools.partial(project_conv_kernel, dims),
             grid_spec=pltpu.PrefetchScalarGridSpec(
-                num_scalar_prefetch=1, grid=(n_groups, 2),
+                num_scalar_prefetch=1, grid=(n_groups,),
                 in_specs=[
                     any_spec, any_spec, any_spec, any_spec,
-                    pl.BlockSpec((4, conv_cols), lambda g, i, tp: (0, g)),
-                    pl.BlockSpec((1, conv_cols), lambda g, i, tp: (0, g)),
-                    pl.BlockSpec((2, LANES), lambda g, i, tp: (0, 0)),
-                    pl.BlockSpec((LANES, group_inner), lambda g, i, tp: (0, g)),
+                    pl.BlockSpec((4, conv_cols), lambda g, tp: (0, g)),
+                    pl.BlockSpec((1, conv_cols), lambda g, tp: (0, g)),
+                    pl.BlockSpec((2, LANES), lambda g, tp: (0, 0)),
+                    pl.BlockSpec((LANES, group_inner), lambda g, tp: (0, g)),
                 ],
                 out_specs=[
-                    pl.BlockSpec((half, conv_cols), lambda g, i, tp: (i, g)),
-                    pl.BlockSpec((3, rows, LANES), lambda g, i, tp: (0, 0, 0), **once),
-                    pl.BlockSpec((n_pieces, depth + PIECE_PAD, LANES), lambda g, i, tp: (0, 0, 0), **once),
+                    pl.BlockSpec((rows, conv_cols), lambda g, tp: (0, g)),
+                    pl.BlockSpec((3, rows, LANES), lambda g, tp: (0, 0, 0), **once),
+                    pl.BlockSpec((n_pieces, depth + PIECE_PAD, LANES), lambda g, tp: (0, 0, 0), **once),
                 ],
                 scratch_shapes=[
                     pltpu.VMEM((2, HALO + half, width), BF16),

time: 206 us -> 201 us (0.976)
  Pallas kernels: 183 us -> 178 us
    pallas_call x1, Pallas kernels: 68.6 us -> 66 us  [layer_block(): pl.pallas_call(functools.partial(project_conv_kernel, dims), grid_spec=pl...]
    pallas_call x1, Pallas kernels: 66.1 us -> 63.9 us  [layer_block(): pl.pallas_call(functools.partial(gate_ssd_kernel, dims, sp_size), grid=(n...]
where the time goes in v4:
time: 201 us
  Pallas kernels  178 us (89%)
  local copies, waits for them, and re-layouts  11.7 us (6%)
  starting transfers between devices  7.62 us (4%)
  other arithmetic  3.6 us (2%)
    pallas_call x1, Pallas kernels, layer_block(): pl.pallas_call(functools.partial(project_conv_kernel, dims), grid_spec=pl...  66 us
    pallas_call x1, Pallas kernels, layer_block(): pl.pallas_call(functools.partial(gate_ssd_kernel, dims, sp_size), grid=(n...  63.9 us
    pallas_call x1, Pallas kernels, layer_block(): pl.pallas_call(functools.partial(gate_out_kernel, dims), grid=(2 * n_tile...  47.8 us
    unnamed x3, local copies, waits for them, and re-layouts  6.63 us
  transfers between devices with their start and end apart: 3, of which 0 were waited for; matrix products, arithmetic and copies ran while one was open for 5% of the time, Pallas kernels for 0%

profile of v4, /device:TPU:1, one launch (start us, length us, event | category | flops | bytes accessed | tf_op | source)
XLA Modules:
  0.0 200.7 jit_solution(1752341362807180673)
XLA Ops:
  0.0 1.4 collective-permute-start
  1.4 0.9 slice.3
  2.3 3.1 %collective-permute-start.1 = (bf16[16,2688]{1,0:T(8,128)(2,1)S(1)}, bf16[16,2688]{1,0:T(8,128)(2,1)S(1)}, u32[]{:S(2)}, u32[]{:S(2)}) collective-permute-start(bf16[16,2688]{1,0:T(8,128)(2,1)S(1)} %slice.3), channel_id=1, source_target_pairs={{1,2},{3,4},{5,6},{7,8},{9,10},{11,12},{13,14},{15,16},{17,18},{19... | collective-permute-start | bytes 258056 | tf_op jit(solution)/shard_map/ppermute | solution.py:424
  5.4 3.1 %collective-permute-start.2 = (bf16[16,2688]{1,0:T(8,128)(2,1)S(1)}, bf16[16,2688]{1,0:T(8,128)(2,1)S(1)}, u32[]{:S(2)}, u32[]{:S(2)}) collective-permute-start(bf16[16,2688]{1,0:T(8,128)(2,1)S(1)} %slice.3), channel_id=1, source_target_pairs={{1,3},{3,5},{5,7},{7,9},{9,11},{11,13},{13,15},{15,17},{17,19},{19... | collective-permute-start | bytes 258056 | tf_op jit(solution)/shard_map/ppermute | solution.py:424
  8.5 0.7 convert_bitcast_fusion
  9.3 0.6 copy.10
  9.9 0.7 convert_bitcast_fusion.1
  10.6 0.6 copy.11
  11.2 0.7 tile.4
  11.9 0.1 broadcast_in_dim_tile.6
  12.0 0.7 tile.5
  12.6 0.1 broadcast_in_dim_tile.7
  12.7 0.7 broadcast_in_dim.13
  13.4 0.7 broadcast_in_dim_reshape.3.ds_ref
  14.1 1.3 broadcast_in_dim.14.nw_ref
  15.4 0.9 compare_convert_fusion.oh_ref
  16.3 0.6 pad_maximum_fusion.hp_ref
  16.9 0.0 collective-permute-done.1
  16.9 0.0 collective-permute-done.2
  16.9 0.6 add.22.halo_ref
  17.6 0.0 collective-permute-done.oth_ref
  17.6 66.0 %project_conv_states.1 = (bf16[2048,3072]{1,0:T(8,128)(2,1)}, f32[3,2048,128]{2,1,0:T(8,128)}, f32[64,40,128]{2,1,0:T(8,128)}) custom-call(s32[1]{0:T(128)} %bitcast.tp_ref, bf16[1024,2688]{1,0:T(8,128)(2,1)} %tok_ref.1, bf16[1024,2688]{1,0:T(8,128)(2,1)} %collective-permute-done.oth_ref, bf16[16,2688]{1,0:T(8,128)(2,1)} %add.22.halo_ref, ...), custom_call_target="tpu_custom_call" | custom-call | flops 33822867456 | bytes 16515072 | tf_op jit(solution)/shard_map/project_conv_states/pallas_call | solution.py:437
  83.6 63.9 %gate_ssd_exchange.1 = (bf16[2,1024,2048]{2,1,0:T(8,128)(2,1)}, f32[2048,2048]{1,0:T(8,128)}, f32[64,32,128]{2,1,0:T(8,128)}) custom-call(f32[64,40,128]{2,1,0:T(8,128)} %get-tuple-element.11.end_ref, bf16[1024,2688]{1,0:T(8,128)(2,1)} %tok_ref.1, bf16[1024,2688]{1,0:T(8,128)(2,1)} %collective-permute-done.oth_ref, bf16[5152,2688]{1,0:T(8,128)(2,1)} %bitcast.10, ...), custom_call_target="tpu_custom_call" | custom-call | tf_op jit(solution)/shard_map/gate_ssd_exchange/pallas_call | solution.py:485
  147.5 47.8 %gate_out_swap.1 = bf16[1024,2688]{1,0:T(8,128)(2,1)} custom-call(f32[2048,2048]{1,0:T(8,128)} %get-tuple-element.14.y_ref, bf16[2048,3072]{1,0:T(8,128)(2,1)} %get-tuple-element.12.act_ref.c0_ref.c1_ref.c2_ref.c3_ref, bf16[2048,3072]{1,0:T(8,128)(2,1)} %get-tuple-element.12.act_ref.c0_ref.c1_ref.c2_ref.c3_ref, ...), custom_call_target="tpu_custom_call" | custom-call | tf_op jit(solution)/shard_map/gate_out_swap/pallas_call | solution.py:539
  195.3 5.4 %copy.13 = bf16[1024,2688]{1,0:T(8,128)(2,1)} copy(bf16[1024,2688]{1,0:T(8,128)(2,1)} %gate_out_swap.1) | data formatting | bytes 11010048
  (2 shorter events, 0.0 us)
Async XLA Ops:
  0.0 17.6 %collective-permute-start = (bf16[1024,2688]{1,0:T(8,128)(2,1)}, bf16[1024,2688]{1,0:T(8,128)(2,1)}, u32[]{:S(2)}, u32[]{:S(2)}) collective-permute-start(bf16[1024,2688]{1,0:T(8,128)(2,1)} %tok_ref.1), channel_id=1, source_target_pairs={{0,1},{1,0},{2,3},{3,2},{4,5},{5,4},{6,7},{7,6},{8,9},{9,8},{10,11... | collective-permute-start | bytes 16515080 | tf_op jit(solution)/shard_map/ppermute | solution.py:420
  2.3 14.7 %collective-permute-start.1 = (bf16[16,2688]{1,0:T(8,128)(2,1)S(1)}, bf16[16,2688]{1,0:T(8,128)(2,1)S(1)}, u32[]{:S(2)}, u32[]{:S(2)}) collective-permute-start(bf16[16,2688]{1,0:T(8,128)(2,1)S(1)} %slice.3), channel_id=1, source_target_pairs={{1,2},{3,4},{5,6},{7,8},{9,10},{11,12},{13,14},{15,16},{17,18},{19... | collective-permute-start | bytes 258056 | tf_op jit(solution)/shard_map/ppermute | solution.py:424
  5.4 11.5 %collective-permute-start.2 = (bf16[16,2688]{1,0:T(8,128)(2,1)S(1)}, bf16[16,2688]{1,0:T(8,128)(2,1)S(1)}, u32[]{:S(2)}, u32[]{:S(2)}) collective-permute-start(bf16[16,2688]{1,0:T(8,128)(2,1)S(1)} %slice.3), channel_id=1, source_target_pairs={{1,3},{3,5},{5,7},{7,9},{9,11},{11,13},{13,15},{15,17},{17,19},{19... | collective-permute-start | bytes 258056 | tf_op jit(solution)/shard_map/ppermute | solution.py:424

commit v5 on v4

--- a/solution.py
+++ b/solution.py
@@ -2,6 +2,7 @@
 
 import jax
 import jax.numpy as jnp
+import numpy as np
 from jax import lax
 from jax.experimental import pallas as pl
 from jax.experimental.pallas import tpu as pltpu
@@ -42,7 +43,7 @@
 
 
 def project_conv_kernel(dims, tp_ref, own_ref, oth_ref, halo_ref, wt_ref,
-                        cw_ref, cb_ref, hp_ref, oh_ref, act_ref, dts_ref, end_ref,
+                        cw_ref, cb_ref, al_ref, db_ref, oh_ref, act_ref, dts_ref, end_ref, held_ref,
                         x_buf, weights, w_dt, ext0, ext1, ext2, ext3, state, total, sems, wsems, dsems):
     n_groups, group_inner, n_state, head_rep, half = dims
     group_id = pl.program_id(0)
@@ -100,8 +101,8 @@
             at = pl.ds(pl.multiple_of(HALO + s * SUB, 16), SUB)
             raw = lax.dot_general(x_buf[half_id, at, :], w_dt[...], CONTRACT_LAST, preferred_element_type=F32).astype(BF16).astype(F32)
             raw = raw + pltpu.roll(raw, n_heads, 1) + pltpu.roll(raw, 2 * n_heads, 1) + pltpu.roll(raw, 3 * n_heads, 1)
-            dt_step = jax.nn.softplus(raw + hp_ref[1:2])
-            log_decay = -jnp.exp(hp_ref[0:1]) * dt_step * LOG2E
+            dt_step = jax.nn.softplus(raw + jnp.concatenate([db_ref[...]] * 4, axis=1))
+            log_decay = -jnp.exp(jnp.concatenate([al_ref[...]] * 4, axis=1)) * dt_step * LOG2E
             row_id = lax.broadcasted_iota(jnp.int32, (SEG, SEG), 0)
             col_id = lax.broadcasted_iota(jnp.int32, (SEG, SEG), 1)
             tri = (row_id >= col_id).astype(F32)
@@ -156,7 +157,9 @@
         for q in range(SUB // SEG):
             lo, hi = q * SEG, (q + 1) * SEG
             new = lax.dot_general(b_all[lo:hi], weighted[lo:hi], (((0,), (0,)), ((), ())), preferred_element_type=F32)
-            state[...] = state[...] * decay[8 * q:8 * q + 1] + new
+            before = state[...]
+            held_ref[(half_id * half + s * SUB) // SEG + q] = before.astype(BF16)
+            state[...] = before * decay[8 * q:8 * q + 1] + new
 
     order = [(h, s) for h in range(2) for s in range(half // SUB)]
     matmul(*order[0])
@@ -182,8 +185,8 @@
             end_ref[piece, depth:depth + PIECE_PAD] = decay[:, t * LANES:(t + 1) * LANES]
 
 
-def gate_ssd_kernel(dims, sp_size, end_ref, own_ref, oth_ref, wt_ref, act_ref, dts_ref, oh_ref, ds_ref, z_ref, y_ref, in_ref,
-                    x_buf, weights, state, gathered, starts, received, xsems, wsems, send_sem, recv_sem, send_sem2, recv_sem2):
+def gate_ssd_kernel(dims, sp_size, end_ref, own_ref, oth_ref, wt_ref, act_ref, dts_ref, held_ref, oh_ref, ds_ref, z_ref, y_ref, in_ref,
+                    x_buf, weights, gathered, starts, received, xsems, wsems, send_sem, recv_sem, send_sem2, recv_sem2):
     n_groups, group_inner, n_state, head_rep, half = dims
     conv_cols = group_inner + 2 * n_state
     group_cols = 2 * group_inner + 2 * n_state + head_rep
@@ -225,11 +228,7 @@
 
         lax.fori_loop(1, sp_size, send_out, 0)
 
-    @pl.when(step_id == n_z)
-    def _():
-        state[...] = jnp.zeros_like(state)
-
-    @pl.when(step_id == n_z + 2)
+    @pl.when(step_id == n_z + 1)
     def _():
         pltpu.make_async_copy(end_ref.at[others, sent], gathered.at[others, sent], recv_sem).wait()
         pltpu.make_async_copy(end_ref.at[others, sent], gathered.at[others, sent], send_sem).wait()
@@ -269,12 +268,10 @@
 
         z_ref[0] = lax.dot_general(x_buf[slot], weights[lax.rem(group_id, 2)], CONTRACT_LAST, preferred_element_type=F32).astype(BF16)
 
-    @pl.when(step_id >= n_z)
-    def _():
-        dt_step = dts_ref[0]
-        cum = dts_ref[1]
-        seg_total = cum[SEG - 1:SEG]
-        end_v = jnp.exp2(seg_total - cum) * dt_step
+    def segment(q):
+        at = slice(q * SEG, (q + 1) * SEG)
+        dt_step = dts_ref[0, at]
+        cum = dts_ref[1, at]
         start_v = jnp.exp2(cum)
         lane = lax.broadcasted_iota(jnp.int32, (SEG, LANES), 1)
         flipped = jnp.where(lane < n_heads, cum, dt_step).T
@@ -285,15 +282,13 @@
         for g in range(n_groups):
             c0 = g * conv_cols
             i0, i1 = g * group_inner, (g + 1) * group_inner
-            x_mat = act_ref[:, c0:c0 + group_inner]
-            end_w = spread(end_v, oh_ref[:, i0:i1])
+            x_mat = act_ref[at, c0:c0 + group_inner]
             from_start = spread(start_v, oh_ref[:, i0:i1])
-            b_mat = act_ref[:, c0 + group_inner:c0 + group_inner + n_state]
-            c_mat = act_ref[:, c0 + group_inner + n_state:c0 + conv_cols]
+            b_mat = act_ref[at, c0 + group_inner:c0 + group_inner + n_state]
+            c_mat = act_ref[at, c0 + group_inner + n_state:c0 + conv_cols]
             c_dot_b = lax.dot_general(c_mat, b_mat, (((1,), (1,)), ((), ())), preferred_element_type=F32)
-            held = state[:, i0:i1]
             x_wide = x_mat.astype(F32)
-            y_rest = jnp.dot(c_mat, held.astype(BF16), preferred_element_type=F32) * from_start + ds_ref[0:1, i0:i1] * x_wide
+            y_rest = jnp.dot(c_mat, held_ref[q, :, i0:i1], preferred_element_type=F32) * from_start + ds_ref[0:1, i0:i1] * x_wide
             for pair in range(head_rep // 2):
                 scores = []
                 for h in (g * head_rep + 2 * pair, g * head_rep + 2 * pair + 1):
@@ -304,10 +299,12 @@
                 zero = jnp.zeros_like(x_pair)
                 x_both = jnp.concatenate([jnp.where(first_half, x_pair, zero), jnp.where(first_half, zero, x_pair)], axis=0)
                 y_diag = jnp.dot(jnp.concatenate(scores, axis=1), x_both, preferred_element_type=F32)
-                y_ref[:, i0 + pair * LANES:i0 + (pair + 1) * LANES] = y_rest[:, pair * LANES:(pair + 1) * LANES] + y_diag
-            weighted = (x_wide * end_w).astype(BF16)
-            new = lax.dot_general(b_mat, weighted, (((0,), (0,)), ((), ())), preferred_element_type=F32)
-            state[:, i0:i1] = held * from_start[SEG - 1:SEG] + new
+                y_ref[at, i0 + pair * LANES:i0 + (pair + 1) * LANES] = y_rest[:, pair * LANES:(pair + 1) * LANES] + y_diag
+
+    @pl.when(step_id >= n_z)
+    def _():
+        for q in range(SUB // SEG):
+            segment(q)
 
     @pl.when(step_id == pl.num_programs(0) - 1)
     def _():
@@ -423,18 +420,17 @@
         edge_same = [(2 * i + 1, 2 * i + 3) for i in range(sp_size - 1)]
         halo = lax.ppermute(tail, ("sp", "tp"), edge) + lax.ppermute(tail, ("sp", "tp"), edge_same)
 
-        head_par = jnp.concatenate([jnp.tile(a_log, 4)[None], jnp.tile(dt_bias, 4)[None]], axis=0)
         skip_row = jnp.repeat(d_skip, head_dim)[None]
-        head_of = jnp.arange(inner_dim) // head_dim
-        lane_head = jnp.where(jnp.arange(LANES) < 3 * n_heads, jnp.arange(LANES) % n_heads, -1)
-        one_hot = (lane_head[:, None] == head_of[None, :]).astype(BF16)
+        head_of = np.arange(inner_dim) // head_dim
+        lane_head = np.where(np.arange(LANES) < 3 * n_heads, np.arange(LANES) % n_heads, -1)
+        one_hot = jnp.asarray(lane_head[:, None] == head_of[None, :], BF16)
         cw = conv_w.reshape(4, all_conv).astype(F32)
         cb = conv_bias.reshape(1, all_conv).astype(F32)
 
         n_pieces = sp_size
         depth = n_state * inner_dim // LANES // n_pieces
         once = dict(pipeline_mode=pl.Buffered(buffer_count=1))
-        act, dts, end_state = pl.pallas_call(
+        act, dts, end_state, held = pl.pallas_call(
             functools.partial(project_conv_kernel, dims),
             grid_spec=pltpu.PrefetchScalarGridSpec(
                 num_scalar_prefetch=1, grid=(n_groups,),
@@ -442,13 +438,15 @@
                     any_spec, any_spec, any_spec, any_spec,
                     pl.BlockSpec((4, conv_cols), lambda g, tp: (0, g)),
                     pl.BlockSpec((1, conv_cols), lambda g, tp: (0, g)),
-                    pl.BlockSpec((2, LANES), lambda g, tp: (0, 0)),
+                    pl.BlockSpec((1, n_heads), lambda g, tp: (0, 0)),
+                    pl.BlockSpec((1, n_heads), lambda g, tp: (0, 0)),
                     pl.BlockSpec((LANES, group_inner), lambda g, tp: (0, g)),
                 ],
                 out_specs=[
                     pl.BlockSpec((rows, conv_cols), lambda g, tp: (0, g)),
                     pl.BlockSpec((3, rows, LANES), lambda g, tp: (0, 0, 0), **once),
                     pl.BlockSpec((n_pieces, depth + PIECE_PAD, LANES), lambda g, tp: (0, 0, 0), **once),
+                    pl.BlockSpec((rows // SEG, n_state, group_inner), lambda g, tp: (0, 0, g)),
                 ],
                 scratch_shapes=[
                     pltpu.VMEM((2, HALO + half, width), BF16),
@@ -468,11 +466,12 @@
                 jax.ShapeDtypeStruct((rows, all_conv), BF16),
                 jax.ShapeDtypeStruct((3, rows, LANES), F32),
                 jax.ShapeDtypeStruct((n_pieces, depth + PIECE_PAD, LANES), F32),
+                jax.ShapeDtypeStruct((rows // SEG, n_state, inner_dim), BF16),
             ],
             compiler_params=pltpu.CompilerParams(vmem_limit_bytes=limit),
             cost_estimate=pl.CostEstimate(flops=2 * rows * width * all_conv, bytes_accessed=2 * width * all_conv, transcendentals=0),
             name="project_conv_states",
-        )(tp_arr, tokens, other, halo, w_in_t, cw, cb, head_par, one_hot)
+        )(tp_arr, tokens, other, halo, w_in_t, cw, cb, a_log[None], dt_bias[None], one_hot)
 
         n_z = 2 * n_groups
 
@@ -484,18 +483,19 @@
 
         gate_z, y_local, incoming = pl.pallas_call(
             functools.partial(gate_ssd_kernel, dims, sp_size),
-            grid=(n_z + rows // SEG,),
+            grid=(n_z + rows // SUB,),
             in_specs=[
                 pl.BlockSpec((n_pieces, depth + PIECE_PAD, LANES), lambda i: (0, 0, 0), **once),
                 any_spec, any_spec, any_spec,
-                pl.BlockSpec((SEG, all_conv), lambda i: (seg_at(i), 0)),
-                pl.BlockSpec((2, SEG, LANES), lambda i: (0, seg_at(i), 0)),
+                pl.BlockSpec((SUB, all_conv), lambda i: (seg_at(i), 0)),
+                pl.BlockSpec((2, SUB, LANES), lambda i: (0, seg_at(i), 0)),
+                pl.BlockSpec((SUB // SEG, n_state, inner_dim), lambda i: (seg_at(i), 0, 0)),
                 pl.BlockSpec((LANES, inner_dim), lambda i: (0, 0), **once),
                 pl.BlockSpec((1, inner_dim), lambda i: (0, 0)),
             ],
             out_specs=[
                 pl.BlockSpec((1, half, group_inner), lambda i: (lax.rem(z_at(i), 2), 0, z_at(i) // 2)),
-                pl.BlockSpec((SEG, inner_dim), lambda i: (seg_at(i), 0)),
+                pl.BlockSpec((SUB, inner_dim), lambda i: (seg_at(i), 0)),
                 pl.BlockSpec((n_pieces, depth, LANES), lambda i: (0, 0, 0), **once),
             ],
             out_shape=[
@@ -506,7 +506,6 @@
             scratch_shapes=[
                 pltpu.VMEM((2, half, width), BF16),
                 pltpu.VMEM((2, group_inner, width), BF16),
-                pltpu.VMEM((n_state, inner_dim), F32),
                 pltpu.VMEM((n_pieces, depth + PIECE_PAD, LANES), F32),
                 pltpu.VMEM((n_pieces, depth, LANES), F32),
                 pltpu.VMEM((n_pieces, depth, LANES), F32),
@@ -517,7 +516,7 @@
             ],
             compiler_params=pltpu.CompilerParams(vmem_limit_bytes=limit, collective_id=0, has_side_effects=True),
             name="gate_ssd_exchange",
-        )(end_state, tokens, other, w_in_t, act, dts, one_hot, skip_row)
+        )(end_state, tokens, other, w_in_t, act, dts, held, one_hot, skip_row)
 
         n_tiles = half // SUB
 

time: 201 us -> 193 us (0.960)
  Pallas kernels: 178 us -> 173 us
    pallas_call x1, Pallas kernels: 63.9 us -> 57.9 us  [layer_block(): pl.pallas_call(functools.partial(gate_ssd_kernel, dims, sp_size), grid=(n...]
  transfers between devices with their start and end apart: 3 -> 3, of which waited for: 0 -> 0; matrix products, arithmetic and copies ran while one was open for 5% -> 4% of each run, Pallas kernels for 0% -> 0%
where the time goes in v5:
time: 193 us
  Pallas kernels  173 us (90%)
  local copies, waits for them, and re-layouts  10.2 us (5%)
  starting transfers between devices  7.62 us (4%)
  other arithmetic  2.1 us (1%)
    pallas_call x1, Pallas kernels, layer_block(): pl.pallas_call(functools.partial(project_conv_kernel, dims), grid_spec=pl...  67.2 us
    pallas_call x1, Pallas kernels, layer_block(): pl.pallas_call(functools.partial(gate_ssd_kernel, dims, sp_size), grid=(n...  57.9 us
    pallas_call x1, Pallas kernels, layer_block(): pl.pallas_call(functools.partial(gate_out_kernel, dims), grid=(2 * n_tile...  47.8 us
    unnamed x3, local copies, waits for them, and re-layouts  6.62 us
  transfers between devices with their start and end apart: 3, of which 0 were waited for; matrix products, arithmetic and copies ran while one was open for 4% of the time, Pallas kernels for 0%

profile of v5, /device:TPU:1, one launch (start us, length us, event | category | flops | bytes accessed | tf_op | source)
XLA Modules:
  0.0 192.8 jit_solution(6217166010089530662)
XLA Ops:
  0.0 1.4 collective-permute-start
  1.4 0.9 slice.3
  2.3 3.1 %collective-permute-start.1 = (bf16[16,2688]{1,0:T(8,128)(2,1)S(1)}, bf16[16,2688]{1,0:T(8,128)(2,1)S(1)}, u32[]{:S(2)}, u32[]{:S(2)}) collective-permute-start(bf16[16,2688]{1,0:T(8,128)(2,1)S(1)} %slice.3), channel_id=1, source_target_pairs={{1,2},{3,4},{5,6},{7,8},{9,10},{11,12},{13,14},{15,16},{17,18},{19... | collective-permute-start | bytes 258056 | tf_op jit(solution)/shard_map/ppermute | solution.py:421
  5.4 3.1 %collective-permute-start.2 = (bf16[16,2688]{1,0:T(8,128)(2,1)S(1)}, bf16[16,2688]{1,0:T(8,128)(2,1)S(1)}, u32[]{:S(2)}, u32[]{:S(2)}) collective-permute-start(bf16[16,2688]{1,0:T(8,128)(2,1)S(1)} %slice.3), channel_id=1, source_target_pairs={{1,3},{3,5},{5,7},{7,9},{9,11},{11,13},{13,15},{15,17},{17,19},{19... | collective-permute-start | bytes 258056 | tf_op jit(solution)/shard_map/ppermute | solution.py:421
  8.5 0.7 convert_bitcast_fusion
  9.3 0.7 convert_bitcast_fusion.1
  10.0 0.6 copy.11
  10.6 0.6 copy.12
  11.2 0.7 broadcast_in_dim.14
  11.9 0.7 broadcast_in_dim_reshape.3.ds_ref
  12.6 1.3 broadcast_in_dim.15.nw_ref
  13.9 0.0 collective-permute-done.1
  13.9 0.0 collective-permute-done.2
  13.9 0.7 add.3.halo_ref
  14.6 0.0 collective-permute-done.oth_ref
  14.6 67.2 %project_conv_states.1 = (bf16[2048,3072]{1,0:T(8,128)(2,1)}, f32[3,2048,128]{2,1,0:T(8,128)}, f32[64,40,128]{2,1,0:T(8,128)}, bf16[16,128,2048]{2,1,0:T(8,128)(2,1)}) custom-call(s32[1]{0:T(128)} %bitcast.tp_ref, bf16[1024,2688]{1,0:T(8,128)(2,1)} %tok_ref.1, bf16[1024,2688]{1,0:T(8,128)(2,1)} %collective-permute-done.oth_ref, ...), custom_call_target="tpu_custom_call" | custom-call | flops 33822867456 | bytes 16515072 | tf_op jit(solution)/shard_map/project_conv_states/pallas_call | solution.py:433
  81.7 57.9 %gate_ssd_exchange.1 = (bf16[2,1024,2048]{2,1,0:T(8,128)(2,1)}, f32[2048,2048]{1,0:T(8,128)}, f32[64,32,128]{2,1,0:T(8,128)}) custom-call(f32[64,40,128]{2,1,0:T(8,128)} %get-tuple-element.12.end_ref, bf16[1024,2688]{1,0:T(8,128)(2,1)} %tok_ref.1, bf16[1024,2688]{1,0:T(8,128)(2,1)} %collective-permute-done.oth_ref, bf16[5152,2688]{1,0:T(8,128)(2,1)} %bitcast.12, ...), custom_call_target="tpu_custom_call" | custom-call | tf_op jit(solution)/shard_map/gate_ssd_exchange/pallas_call | solution.py:484
  139.7 47.8 %gate_out_swap.1 = bf16[1024,2688]{1,0:T(8,128)(2,1)} custom-call(f32[2048,2048]{1,0:T(8,128)} %get-tuple-element.16.y_ref, bf16[2048,3072]{1,0:T(8,128)(2,1)} %get-tuple-element.13.act_ref.c0_ref.c1_ref.c2_ref.c3_ref, bf16[2048,3072]{1,0:T(8,128)(2,1)} %get-tuple-element.13.act_ref.c0_ref.c1_ref.c2_ref.c3_ref, ...), custom_call_target="tpu_custom_call" | custom-call | tf_op jit(solution)/shard_map/gate_out_swap/pallas_call | solution.py:538
  187.4 5.4 %copy.14 = bf16[1024,2688]{1,0:T(8,128)(2,1)} copy(bf16[1024,2688]{1,0:T(8,128)(2,1)} %gate_out_swap.1) | data formatting | bytes 11010048
Async XLA Ops:
  0.0 14.6 %collective-permute-start = (bf16[1024,2688]{1,0:T(8,128)(2,1)}, bf16[1024,2688]{1,0:T(8,128)(2,1)}, u32[]{:S(2)}, u32[]{:S(2)}) collective-permute-start(bf16[1024,2688]{1,0:T(8,128)(2,1)} %tok_ref.1), channel_id=1, source_target_pairs={{0,1},{1,0},{2,3},{3,2},{4,5},{5,4},{6,7},{7,6},{8,9},{9,8},{10,11... | collective-permute-start | bytes 16515080 | tf_op jit(solution)/shard_map/ppermute | solution.py:417
  2.3 11.6 %collective-permute-start.1 = (bf16[16,2688]{1,0:T(8,128)(2,1)S(1)}, bf16[16,2688]{1,0:T(8,128)(2,1)S(1)}, u32[]{:S(2)}, u32[]{:S(2)}) collective-permute-start(bf16[16,2688]{1,0:T(8,128)(2,1)S(1)} %slice.3), channel_id=1, source_target_pairs={{1,2},{3,4},{5,6},{7,8},{9,10},{11,12},{13,14},{15,16},{17,18},{19... | collective-permute-start | bytes 258056 | tf_op jit(solution)/shard_map/ppermute | solution.py:421
  5.4 8.5 %collective-permute-start.2 = (bf16[16,2688]{1,0:T(8,128)(2,1)S(1)}, bf16[16,2688]{1,0:T(8,128)(2,1)S(1)}, u32[]{:S(2)}, u32[]{:S(2)}) collective-permute-start(bf16[16,2688]{1,0:T(8,128)(2,1)S(1)} %slice.3), channel_id=1, source_target_pairs={{1,3},{3,5},{5,7},{7,9},{9,11},{11,13},{13,15},{15,17},{17,19},{19... | collective-permute-start | bytes 258056 | tf_op jit(solution)/shard_map/ppermute | solution.py:421
